TPU v7x, 32 devices: a whole 2x2x4 slice. The times are simulated.
32 devices in a mesh: wide: 8 (over z, x), narrow: 4 (over y, core).
Axes of the slice: x: 2, y: 2, z: 4, core: 2. Of those that a mesh axis runs over, the one named last changes fastest.
Arguments:
- old_basis: float32 [16, 2048, 512], P(None, ('wide', 'narrow')), may hold values from -6 to 6
- restart_coeffs: float32 [16], replicated, may hold values from -1 to 1
- geometry: float32 [4, 2048, 512], P(None, ('wide', 'narrow')), may hold values from 0.01 to 18, as said below
- orientation: int32 [6, 2048], P(None, ('wide', 'narrow')), may hold values from 0 to 7
Outputs:
- new_basis: float32 [2, 2048, 512], P(None, ('wide', 'narrow'))
- hessenberg: float32 [2, 18], replicated
Inputs may be any that keep to these rules, and one draw needn't show every extreme that they name: `geometry`: every entry is positive.
All inputs are finite; a program needn't handle non-finite values.
Results may differ from a plain program's by a relative error of at most 0.0003.
Values sent between devices are 32-bit elements; how exact they have to be, the bound alone decides.
A program may use at most 64 MiB of HBM per device.

v0:
```python
import functools

import jax
import jax.numpy as jnp
import numpy as np
from jax import lax
from jax.experimental import pallas as pl
from jax.experimental.pallas import tpu as pltpu
from jax.sharding import PartitionSpec as P

NP = 8
EX = 4
EY = 4
EZ = 4
LANES = 128
FACE = NP * NP
MESH = pl.DeviceIdType.MESH
highest = lax.Precision.HIGHEST
epsilon = 1e-06


def legendre_columns(nodes, degree):
    columns = [nodes * 0.0 + 1.0, nodes * 1.0]
    for order in range(2, degree + 1):
        columns.append(
            ((2 * order - 1) * nodes * columns[order - 1] - (order - 1) * columns[order - 2])
            / order
        )
    return columns


def gll_derivative(extent):
    degree = extent - 1
    nodes = np.cos(np.pi * np.arange(extent) / degree)
    for sweep in range(100):
        columns = legendre_columns(nodes, degree)
        nodes = nodes - (nodes * columns[degree] - columns[degree - 1]) / (extent * columns[degree])
    gll_nodes = nodes[::-1] * 1.0
    values = legendre_columns(gll_nodes, degree)[degree]
    matrix = np.zeros((extent, extent))
    for row_idx in range(extent):
        for col_idx in range(extent):
            if row_idx != col_idx:
                matrix[row_idx, col_idx] = values[row_idx] / (
                    values[col_idx] * (gll_nodes[row_idx] - gll_nodes[col_idx])
                )
    matrix[0, 0] = -degree * (degree + 1) / 4.0
    matrix[extent - 1, extent - 1] = degree * (degree + 1) / 4.0
    return matrix


def tables():
    matrix = gll_derivative(NP)
    identity = np.eye(NP)
    pair = np.eye(2)
    along_y = np.kron(pair, np.kron(matrix, identity))
    along_z = np.kron(pair, np.kron(identity, matrix))
    forward = np.concatenate([along_y.T, along_z.T], axis=1)
    backward = np.concatenate([along_y, along_z], axis=0)
    tiles = NP // 2
    coef = np.zeros((2, tiles, tiles, 2, LANES))
    for way, table in enumerate((matrix, matrix.T)):
        for out_tile in range(tiles):
            for in_tile in range(tiles):
                for half in range(2):
                    lanes = slice(half * FACE, (half + 1) * FACE)
                    row = 2 * out_tile + half
                    coef[way, out_tile, in_tile, 0, lanes] = table[row, 2 * in_tile + half]
                    coef[way, out_tile, in_tile, 1, lanes] = table[row, 2 * in_tile + 1 - half]
    return (
        jnp.asarray(forward, jnp.float32),
        jnp.asarray(backward, jnp.float32),
        jnp.asarray(coef.reshape(-1, LANES), jnp.float32),
    )


def pair_rows(kept):
    count = kept + 2
    listed = [(at, kept + 1) for at in range(count)]
    listed += [(at, kept) for at in range(kept + 1)]
    block = 4
    for left in range(0, kept, block):
        for right in range(left, kept, block):
            for one in range(left, left + block):
                for two in range(max(right, one), right + block):
                    listed.append((one, two))
    return -(-len(listed) // LANES), listed


def take_lanes(values, index):
    return jnp.take_along_axis(values, index, axis=1, mode="promise_in_bounds")


def rotated(row, col, code):
    row = row ^ (7 * (code & 1))
    col = col ^ (7 * ((code >> 1) & 1))
    return jnp.where((code & 4) != 0, col * NP + row, row * NP + col)


def kernel(
    n_wide,
    n_narrow,
    coeffs,
    basis_hbm,
    geom_hbm,
    orient,
    forward_hbm,
    backward_hbm,
    coef_hbm,
    pairs_hbm,
    out,
    hess,
    basis,
    geom,
    forward,
    backward,
    coef,
    index,
    orient_pad,
    image,
    first,
    face_y,
    face_z,
    halo_y,
    halo_z,
    outbox,
    inbox,
    pairs,
    row_out,
    row_in,
    pair_out,
    pair_in,
    load_sem,
    halo_send,
    halo_recv,
    row_send,
    row_recv,
):
    wide = lax.axis_index("wide")
    narrow = lax.axis_index("narrow")
    devices = n_wide * n_narrow
    me = wide * n_narrow + narrow
    kept, elements, points = basis.shape
    tiles = points // LANES
    total = float(elements * points * devices)

    def load(source, target, slot):
        return pltpu.make_async_copy(source, target, load_sem.at[slot])

    chunk = kept // 4
    loads = [
        load(basis_hbm.at[pl.ds(part * chunk, chunk)], basis.at[pl.ds(part * chunk, chunk)], part)
        for part in range(4)
    ]
    loads += [
        load(forward_hbm, forward, 4),
        load(geom_hbm, geom, 5),
        load(backward_hbm, backward, 6),
        load(coef_hbm, coef, 7),
        load(pairs_hbm, pairs, 8),
    ]
    for copy in loads:
        copy.start()

    messages = ((row_out, row_in), (pair_out, pair_in))
    inbox[...] = jnp.zeros_like(inbox)

    def peer(step):
        if devices & (devices - 1):
            other = lax.rem(me + step, devices)
        else:
            other = me
            for bit in range(devices.bit_length() - 1):
                if step >> bit & 1:
                    other = other + (1 - 2 * lax.rem(me // 2**bit, 2)) * 2**bit
        return (other // n_narrow, lax.rem(other, n_narrow))

    def each_peer(act):
        if devices <= 64:
            for step in range(devices - 1, 0, -1):
                act(peer(step))
        else:

            def body(step, carry):
                other = lax.rem(me + step, devices)
                act((other // n_narrow, lax.rem(other, n_narrow)))
                return carry

            lax.fori_loop(1, devices, body, 0)

    barrier = pltpu.get_barrier_semaphore()

    def greet(where):
        pl.semaphore_signal(barrier, inc=1, device_id=where, device_id_type=MESH)

    each_peer(greet)

    lane = lax.broadcasted_iota(jnp.int32, (elements, LANES), 1)
    line = lax.broadcasted_iota(jnp.int32, (elements, LANES), 0)
    low_half = lane < FACE
    half = lane // FACE
    mid = (lane // NP) % NP
    fast = lane % NP
    row_y = (line // EZ) % EY
    row_z = line % EZ
    at_y = (mid == 0) | (mid == NP - 1)
    at_z = (fast == 0) | (fast == NP - 1)

    orient_pad[...] = jnp.zeros_like(orient_pad)
    orient_pad[pl.ds(0, 6), pl.ds(0, elements)] = orient[...]
    codes = jnp.transpose(orient_pad[...])[:elements]
    code = [jnp.broadcast_to(codes[:, f : f + 1], (elements, LANES)) for f in range(6)]
    code_x = jnp.where(low_half, code[0], code[1])
    index[2 * tiles] = rotated(mid, fast, code_x) + jnp.where(low_half, FACE, 0)
    code_y = jnp.where(mid == 0, code[2], code[3])
    code_z = jnp.where(fast == 0, code[4], code[5])
    for tile in range(tiles):
        first_pos = 2 * tile + half
        index[tile] = rotated(first_pos, fast, code_y) + jnp.where(mid == 0, FACE, 0)
        index[tiles + tile] = rotated(first_pos, mid, code_z) + jnp.where(fast == 0, FACE, 0)

    pick_y = (mid % 2) * FACE + half * (FACE - NP) + fast
    pick_z = (mid % 2) * FACE + fast * NP + half * (NP - 1)
    source_tile = mid // 2

    def tile_of(values, tile):
        return values[:, tile * LANES : (tile + 1) * LANES]

    def swap(values):
        return pltpu.roll(values, FACE, axis=1)

    def along_x(parts, way):
        swapped = [swap(part) for part in parts]
        outs = []
        for out_tile in range(tiles):
            acc = None
            for in_tile in range(tiles):
                at = ((way * tiles + out_tile) * tiles + in_tile) * 2
                term = (
                    coef[pl.ds(at, 1), :] * parts[in_tile]
                    + coef[pl.ds(at + 1, 1), :] * swapped[in_tile]
                )
                acc = term if acc is None else acc + term
            outs.append(acc)
        return outs

    def local(parts):
        stacked = jnp.concatenate(parts, axis=0)
        grads = jnp.dot(
            stacked, forward[...], precision=highest, preferred_element_type=jnp.float32
        )
        geom_y = jnp.concatenate([geom[1, :, pl.ds(t * LANES, LANES)] for t in range(tiles)], axis=0)
        geom_z = jnp.concatenate([geom[2, :, pl.ds(t * LANES, LANES)] for t in range(tiles)], axis=0)
        flux = jnp.concatenate([grads[:, :LANES] * geom_y, grads[:, LANES:] * geom_z], axis=1)
        back = jnp.dot(
            flux, backward[...], precision=highest, preferred_element_type=jnp.float32
        )
        grad_x = along_x(parts, 0)
        flux_x = [grad_x[t] * geom[0, :, pl.ds(t * LANES, LANES)] for t in range(tiles)]
        back_x = along_x(flux_x, 1)
        return [
            back[t * elements : (t + 1) * elements]
            + back_x[t]
            + geom[3, :, pl.ds(t * LANES, LANES)] * parts[t]
            for t in range(tiles)
        ]

    def faces(parts, pick):
        found = take_lanes(parts[0], pick)
        for tile in range(1, tiles):
            found = jnp.where(source_tile == tile, take_lanes(parts[tile], pick), found)
        return found

    has = (narrow > 0, narrow < n_narrow - 1, wide > 0, wide < n_wide - 1)
    where_to = ((wide, narrow - 1), (wide, narrow + 1), (wide - 1, narrow), (wide + 1, narrow))

    def face_copy(step, side):
        return pltpu.make_async_remote_copy(
            src_ref=outbox.at[step, side],
            dst_ref=inbox.at[step, side ^ 1],
            send_sem=halo_send.at[step, side],
            recv_sem=halo_recv.at[step, side ^ 1],
            device_id=where_to[side],
            device_id_type=MESH,
        )

    def face_arrival(step, side):
        return pltpu.make_async_copy(
            inbox.at[step, side], inbox.at[step, side], halo_recv.at[step, side]
        )

    def operate(parts, step, ready, beside=lambda: None):
        result = local(parts)
        def send_faces(sides):
            for side in sides:

                @pl.when(has[side])
                def _():
                    face_copy(step, side).start()

        found_z = faces(result, pick_z)
        face_z[...] = found_z
        outbox[step, 2] = face_z[pl.ds(0, EX * EY, stride=EZ), :]
        outbox[step, 3] = face_z[pl.ds(EZ - 1, EX * EY, stride=EZ), :]
        ready()
        send_faces((2, 3))
        found_y = faces(result, pick_y)
        face_y[...] = found_y
        for ex in range(EX):
            outbox[step, 0, pl.ds(ex * EZ, EZ), :] = face_y[pl.ds(ex * EY * EZ, EZ), :]
            outbox[step, 1, pl.ds(ex * EZ, EZ), :] = face_y[pl.ds(ex * EY * EZ + (EY - 1) * EZ, EZ), :]
        send_faces((0, 1))

        face_x = jnp.where(low_half, result[0], result[tiles - 1])
        width = EY * EZ
        blank = jnp.zeros((width, LANES), jnp.float32)
        in_x = jnp.where(
            low_half,
            jnp.concatenate([face_x[width:], blank], axis=0),
            jnp.concatenate([blank, face_x[: elements - width]], axis=0),
        )
        in_y = jnp.where(
            low_half, pltpu.roll(found_y, elements - EZ, axis=0), pltpu.roll(found_y, EZ, axis=0)
        )
        in_z = jnp.where(
            low_half, pltpu.roll(found_z, elements - 1, axis=0), pltpu.roll(found_z, 1, axis=0)
        )
        got_x = take_lanes(in_x, index[2 * tiles])
        result[0] = result[0] + jnp.where(low_half, got_x, 0.0)
        result[tiles - 1] = result[tiles - 1] + jnp.where(low_half, 0.0, got_x)

        beside()

        def await_faces(sides):
            for side in sides:

                @pl.when(has[side])
                def _():
                    face_arrival(step, side).wait()

        await_faces((0, 1))
        for ex in range(EX):
            halo_y[pl.ds(ex * EY * EZ, EZ), :] = inbox[step, 0, pl.ds(ex * EZ, EZ), :]
            halo_y[pl.ds(ex * EY * EZ + (EY - 1) * EZ, EZ), :] = inbox[step, 1, pl.ds(ex * EZ, EZ), :]
        edge_y = row_y == jnp.where(low_half, EY - 1, 0)
        in_y = jnp.where(edge_y, halo_y[...], in_y)
        for t in range(tiles):
            result[t] = result[t] + jnp.where(at_y, take_lanes(in_y, index[t]), 0.0)
            image[:, pl.ds(t * LANES, LANES)] = result[t]

        await_faces((2, 3))
        halo_z[pl.ds(0, EX * EY, stride=EZ), :] = inbox[step, 2]
        halo_z[pl.ds(EZ - 1, EX * EY, stride=EZ), :] = inbox[step, 3]
        edge_z = row_z == jnp.where(low_half, EZ - 1, 0)
        in_z = jnp.where(edge_z, halo_z[...], in_z)
        return [
            image[:, pl.ds(t * LANES, LANES)]
            + jnp.where(at_z, take_lanes(in_z, index[tiles + t]), 0.0)
            for t in range(tiles)
        ]

    def folded(values):
        acc = tile_of(values, 0)
        for tile in range(1, tiles):
            acc = acc + tile_of(values, tile)
        return jnp.sum(acc.reshape(elements // 8, 8, LANES), axis=0)

    def to_row(partials, begin=0):
        count = -(-len(partials) // 8) * 8
        rows = [jnp.sum(part, axis=0, keepdims=True) for part in partials]
        rows += [jnp.zeros((1, LANES), jnp.float32)] * (count - len(rows))
        block = jnp.concatenate(rows, axis=0)
        sums = jnp.sum(block, axis=1, keepdims=True)
        place = lax.broadcasted_iota(jnp.int32, (count, LANES), 0) + begin == lax.broadcasted_iota(
            jnp.int32, (count, LANES), 1
        )
        return jnp.sum(jnp.where(place, sums, 0.0), axis=0, keepdims=True)

    def all_sum(block, phase, beside):
        outgoing, incoming = messages[phase]
        outgoing[...] = block
        incoming[pl.ds(me, 1)] = block.reshape((1,) + block.shape)

        def send(where):
            pltpu.make_async_remote_copy(
                src_ref=outgoing,
                dst_ref=incoming.at[me],
                send_sem=row_send.at[phase],
                recv_sem=row_recv.at[phase],
                device_id=where,
                device_id_type=MESH,
            ).start()

        each_peer(send)
        result = beside()
        span = incoming.at[pl.ds(0, devices - 1)]
        pltpu.make_async_copy(span, span, row_recv.at[phase]).wait()
        return jnp.sum(incoming[...], axis=0), result

    def weight(row, at):
        return row[:, at : at + 1]

    start = None
    for part in range(4):
        loads[part].wait()
        for at in range(part * chunk, (part + 1) * chunk):
            term = coeffs[at] * basis[at]
            start = term if start is None else start + term
    for copy in loads[4:]:
        copy.wait()

    def greeted():
        pl.semaphore_wait(barrier, devices - 1)

    image_parts = operate([tile_of(start, t) for t in range(tiles)], 0, greeted)
    for t in range(tiles):
        image[:, pl.ds(t * LANES, LANES)] = image_parts[t]
    rows, listed = pair_rows(kept)
    fresh = 2 * kept + 3

    def gram():
        partials = []
        block = 4
        for left in range(0, kept, block):
            for right in range(left, kept, block):
                wanted = [
                    (one, two)
                    for one in range(left, left + block)
                    for two in range(max(right, one), right + block)
                ]

                def body(step, carry):
                    base = pl.multiple_of(step * 8, 8)
                    carry = list(carry)
                    for tile in range(tiles):
                        at = (pl.ds(base, 8), pl.ds(tile * LANES, LANES))
                        ones = [basis[(left + m,) + at] for m in range(block)]
                        twos = ones if left == right else [
                            basis[(right + m,) + at] for m in range(block)
                        ]
                        for spot, (one, two) in enumerate(wanted):
                            carry[spot] = carry[spot] + ones[one - left] * twos[two - right]
                    return tuple(carry)

                zero = jnp.zeros((8, LANES), jnp.float32)
                partials += list(
                    lax.fori_loop(0, elements // 8, body, (zero,) * len(wanted))
                )
        gram_rows = []
        for begin in range(0, rows * LANES, LANES):
            lo = max(begin, fresh)
            here = partials[lo - fresh : begin + LANES - fresh]
            row = to_row(here, lo - begin) if here else jnp.zeros((1, LANES), jnp.float32)
            gram_rows.append(row)
        return gram_rows

    row = to_row([folded(basis[at] * image[...]) for at in range(kept)])
    sums, gram_part = all_sum(row, 0, gram)
    proj_one = sums / total
    acc = image[...]
    for at in range(kept):
        acc = acc - weight(proj_one, at) * basis[at]
    first[...] = acc

    with_first = []

    def project_first():
        with_first.extend(
            [folded(basis[at] * first[...]) for at in range(kept)]
            + [folded(first[...] * first[...])]
        )

    image_parts = operate(
        [first[:, pl.ds(t * LANES, LANES)] for t in range(tiles)], 1, lambda: None, project_first
    )
    for t in range(tiles):
        image[:, pl.ds(t * LANES, LANES)] = image_parts[t]
    row = to_row(
        [folded(basis[at] * image[...]) for at in range(kept)]
        + [folded(first[...] * image[...]), folded(image[...] * image[...])]
        + with_first
    )
    block = jnp.concatenate([gram_part[0] + row] + gram_part[1:], axis=0)
    sums, _ = all_sum(block, 1, lambda: None)
    sums = sums / total
    along = sums[0:1]
    norm_one = jnp.sqrt(weight(along, fresh - 1) + epsilon)
    scale_one = 1.0 / norm_one
    proj_two = along * scale_one
    self_two = weight(along, kept) * scale_one * scale_one

    spot = lax.broadcasted_iota(jnp.int32, (8, LANES), 1)
    factor = jnp.broadcast_to(along, (8, LANES))
    factor = jnp.where(spot < kept, -factor, 0.0)
    factor = jnp.where(spot == kept, -self_two, factor)
    factor = jnp.where(spot == kept + 1, 1.0, factor)
    square = jnp.zeros((1, LANES), jnp.float32)
    for at in range(rows):
        left = jnp.broadcast_to(pairs[pl.ds(at, 1), :], (8, LANES))
        right = jnp.broadcast_to(pairs[pl.ds(rows + at, 1), :], (8, LANES))
        product = take_lanes(factor, left) * take_lanes(factor, right)
        product = jnp.where(left == right, product, 2.0 * product)
        used = spot + at * LANES < len(listed)
        square = square + jnp.where(used, product * sums[at : at + 1], 0.0)[0:1]
    square = jnp.maximum(jnp.sum(square, axis=1, keepdims=True), 0.0) * (scale_one * scale_one)
    norm_two = jnp.sqrt(square + epsilon)

    acc = image[...] - (self_two * first[...])
    for at in range(kept):
        acc = acc - weight(along, at) * basis[at]
    out[0] = first[...] * scale_one
    out[1] = acc * (scale_one / norm_two)

    spot = lax.broadcasted_iota(jnp.int32, (1, LANES), 1)
    row_first = jnp.where(spot < kept, proj_one, jnp.where(spot == kept, norm_one, 0.0))
    row_second = jnp.where(spot < kept, proj_two, jnp.where(spot == kept, self_two, norm_two))
    hess[pl.ds(0, 1), :] = row_first[:, : kept + 2]
    hess[pl.ds(1, 1), :] = row_second[:, : kept + 2]

    for step in range(2):
        for side in range(4):

            @pl.when(has[side])
            def _():
                face_copy(step, side).wait_send()

    for phase in range(2):
        span = messages[phase][1].at[pl.ds(0, devices - 1)]
        pltpu.make_async_copy(span, span, row_send.at[phase]).wait()


def on_device(n_wide, n_narrow, old_basis, restart_coeffs, geometry, orientation):
    kept, elements, points = old_basis.shape
    tiles = points // LANES
    devices = n_wide * n_narrow
    forward, backward, coef = tables()
    rows, listed = pair_rows(kept)
    pairs = np.zeros((2 * rows, LANES), np.int32)
    for at, (left, right) in enumerate(listed):
        pairs[at // LANES, at % LANES] = left
        pairs[rows + at // LANES, at % LANES] = right
    pairs = jnp.asarray(pairs)
    anywhere = pl.BlockSpec(memory_space=pl.ANY)
    vmem = pl.BlockSpec(memory_space=pltpu.VMEM)
    f32 = jnp.float32
    border = EX * EY
    shapes = ((2, elements, points), (2, kept + 2))
    held = pl.pallas_call(
        functools.partial(kernel, n_wide, n_narrow),
        out_shape=tuple(pltpu.VMEM(shape, f32) for shape in shapes),
        in_specs=[
            pl.BlockSpec(memory_space=pltpu.SMEM),
            anywhere,
            anywhere,
            vmem,
            anywhere,
            anywhere,
            anywhere,
            anywhere,
        ],
        out_specs=(vmem, vmem),
        scratch_shapes=[
            pltpu.VMEM(old_basis.shape, f32),
            pltpu.VMEM(geometry.shape, f32),
            pltpu.VMEM(forward.shape, f32),
            pltpu.VMEM(backward.shape, f32),
            pltpu.VMEM(coef.shape, f32),
            pltpu.VMEM((2 * tiles + 1, elements, LANES), jnp.int32),
            pltpu.VMEM((8, LANES), jnp.int32),
            pltpu.VMEM((elements, points), f32),
            pltpu.VMEM((elements, points), f32),
            pltpu.VMEM((elements, LANES), f32),
            pltpu.VMEM((elements, LANES), f32),
            pltpu.VMEM((elements, LANES), f32),
            pltpu.VMEM((elements, LANES), f32),
            pltpu.VMEM((2, 4, border, LANES), f32),
            pltpu.VMEM((2, 4, border, LANES), f32),
            pltpu.VMEM(pairs.shape, jnp.int32),
            pltpu.VMEM((1, LANES), f32),
            pltpu.VMEM((devices, 1, LANES), f32),
            pltpu.VMEM((rows, LANES), f32),
            pltpu.VMEM((devices, rows, LANES), f32),
            pltpu.SemaphoreType.DMA((9,)),
            pltpu.SemaphoreType.DMA((2, 4)),
            pltpu.SemaphoreType.DMA((2, 4)),
            pltpu.SemaphoreType.DMA((2,)),
            pltpu.SemaphoreType.DMA((2,)),
        ],
        compiler_params=pltpu.CompilerParams(collective_id=0, has_side_effects=True),
        name="arnoldi",
    )(restart_coeffs, old_basis, geometry, orientation, forward, backward, coef, pairs)
    return held


def solution(mesh):
    in_specs = (
        P(None, ("wide", "narrow"), None),
        P(),
        P(None, ("wide", "narrow"), None),
        P(None, ("wide", "narrow")),
    )
    out_specs = (P(None, ("wide", "narrow"), None), P())
    return jax.shard_map(
        functools.partial(on_device, mesh.shape["wide"], mesh.shape["narrow"]),
        mesh=mesh,
        in_specs=in_specs,
        out_specs=out_specs,
        check_vma=False,
    )
```

profile of v0, /device:TPU:0, one launch (start us, length us, event | category | flops | bytes accessed | tf_op | source)
XLA Modules:
  0.0 26.9 jit_solution(15466774315187194281)
XLA Ops:
  0.6 25.0 %arnoldi.1 = (f32[2,64,512]{2,1,0:T(8,128)S(1)}, f32[2,18]{1,0:T(2,128)S(1)}) custom-call(f32[16]{0:T(128)} %coeffs.1, f32[16,64,512]{2,1,0:T(8,128)} %basis_hbm.1, f32[4,64,512]{2,1,0:T(8,128)} %geom_hbm.1, s32[6,64]{1,0:T(8,128)} %orient.1, f32[128,256]{1,0:T(8,128)} %constant.8.clone.forward_hbm, f32[256,128]{1,0:T(8,128)} %constant.9.clone.backward_hbm, ...), custom_call_target="tpu_custom_call" | custom-call | tf_op jit(solution)/shard_map/arnoldi/pallas_call | solution.py:548
  25.7 0.7 %copy.12 = f32[2,64,512]{2,1,0:T(8,128)} copy(f32[2,64,512]{2,1,0:T(8,128)S(1)} %get-tuple-element.2) | data formatting | bytes 524288
  26.4 0.6 %copy.13 = f32[2,18]{1,0:T(2,128)} copy(f32[2,18]{1,0:T(2,128)S(1)} %get-tuple-element.3) | data formatting | bytes 288
where the time goes:
time: 27.1 us; the launch traced here: 26.9 us
  Pallas kernels  25 us (92%)
  local copies, waits for them, and re-layouts  1.27 us (5%)
  between operations  0.64 us (2%)
    pallas_call x1, Pallas kernels, on_device(): pl.pallas_call(functools.partial(kernel, n_wide, n_narrow), out_shape=tup...  25 us
    unnamed x2, local copies, waits for them, and re-layouts  1.27 us

commit v1 on v0

--- a/solution.py
+++ b/solution.py
@@ -49,6 +49,12 @@
     return matrix
 
 
+def halves(table):
+    table = np.asarray(table, np.float32)
+    upper = table.astype(jnp.bfloat16).astype(np.float32)
+    return upper, table - upper
+
+
 def tables():
     matrix = gll_derivative(NP)
     identity = np.eye(NP)
@@ -67,9 +73,11 @@
                     row = 2 * out_tile + half
                     coef[way, out_tile, in_tile, 0, lanes] = table[row, 2 * in_tile + half]
                     coef[way, out_tile, in_tile, 1, lanes] = table[row, 2 * in_tile + 1 - half]
+    ahead, ahead_rest = halves(forward)
+    back, back_rest = halves(backward)
+    packed = np.concatenate([ahead, ahead_rest, np.concatenate([back, back_rest], axis=1)], axis=0)
     return (
-        jnp.asarray(forward, jnp.float32),
-        jnp.asarray(backward, jnp.float32),
+        jnp.asarray(packed, jnp.bfloat16),
         jnp.asarray(coef.reshape(-1, LANES), jnp.float32),
     )
 
@@ -100,20 +108,20 @@
 def kernel(
     n_wide,
     n_narrow,
-    coeffs,
+    coeffs_hbm,
     basis_hbm,
     geom_hbm,
-    orient,
-    forward_hbm,
-    backward_hbm,
+    orient_hbm,
+    packed_hbm,
     coef_hbm,
     pairs_hbm,
     out,
     hess,
+    coeffs,
     basis,
     geom,
-    forward,
-    backward,
+    orient,
+    packed,
     coef,
     index,
     orient_pad,
@@ -152,18 +160,18 @@
         load(basis_hbm.at[pl.ds(part * chunk, chunk)], basis.at[pl.ds(part * chunk, chunk)], part)
         for part in range(4)
     ]
-    loads += [
-        load(forward_hbm, forward, 4),
-        load(geom_hbm, geom, 5),
-        load(backward_hbm, backward, 6),
-        load(coef_hbm, coef, 7),
-        load(pairs_hbm, pairs, 8),
+    load_coeffs = load(coeffs_hbm, coeffs, 4)
+    load_tables = [
+        load(packed_hbm, packed, 5),
+        load(coef_hbm, coef, 6),
+        load(geom_hbm, geom, 7),
     ]
-    for copy in loads:
+    load_orient = load(orient_hbm, orient, 8)
+    load_pairs = load(pairs_hbm, pairs, 9)
+    for copy in [load_coeffs] + loads + load_tables + [load_orient, load_pairs]:
         copy.start()
 
     messages = ((row_out, row_in), (pair_out, pair_in))
-    inbox[...] = jnp.zeros_like(inbox)
 
     def peer(step):
         if devices & (devices - 1):
@@ -193,6 +201,7 @@
     def greet(where):
         pl.semaphore_signal(barrier, inc=1, device_id=where, device_id_type=MESH)
 
+    inbox[...] = jnp.zeros_like(inbox)
     each_peer(greet)
 
     lane = lax.broadcasted_iota(jnp.int32, (elements, LANES), 1)
@@ -206,22 +215,24 @@
     at_y = (mid == 0) | (mid == NP - 1)
     at_z = (fast == 0) | (fast == NP - 1)
 
-    orient_pad[...] = jnp.zeros_like(orient_pad)
-    orient_pad[pl.ds(0, 6), pl.ds(0, elements)] = orient[...]
-    codes = jnp.transpose(orient_pad[...])[:elements]
-    code = [jnp.broadcast_to(codes[:, f : f + 1], (elements, LANES)) for f in range(6)]
-    code_x = jnp.where(low_half, code[0], code[1])
-    index[2 * tiles] = rotated(mid, fast, code_x) + jnp.where(low_half, FACE, 0)
-    code_y = jnp.where(mid == 0, code[2], code[3])
-    code_z = jnp.where(fast == 0, code[4], code[5])
-    for tile in range(tiles):
-        first_pos = 2 * tile + half
-        index[tile] = rotated(first_pos, fast, code_y) + jnp.where(mid == 0, FACE, 0)
-        index[tiles + tile] = rotated(first_pos, mid, code_z) + jnp.where(fast == 0, FACE, 0)
-
     pick_y = (mid % 2) * FACE + half * (FACE - NP) + fast
     pick_z = (mid % 2) * FACE + fast * NP + half * (NP - 1)
     source_tile = mid // 2
+
+    def make_index():
+        load_orient.wait()
+        orient_pad[...] = jnp.zeros_like(orient_pad)
+        orient_pad[pl.ds(0, 6), pl.ds(0, elements)] = orient[...]
+        codes = jnp.transpose(orient_pad[...])[:elements]
+        code = [jnp.broadcast_to(codes[:, f : f + 1], (elements, LANES)) for f in range(6)]
+        code_x = jnp.where(low_half, code[0], code[1])
+        index[2 * tiles] = rotated(mid, fast, code_x) + jnp.where(low_half, FACE, 0)
+        code_y = jnp.where(mid == 0, code[2], code[3])
+        code_z = jnp.where(fast == 0, code[4], code[5])
+        for tile in range(tiles):
+            first_pos = 2 * tile + half
+            index[tile] = rotated(first_pos, fast, code_y) + jnp.where(mid == 0, FACE, 0)
+            index[tiles + tile] = rotated(first_pos, mid, code_z) + jnp.where(fast == 0, FACE, 0)
 
     def tile_of(values, tile):
         return values[:, tile * LANES : (tile + 1) * LANES]
@@ -244,17 +255,27 @@
             outs.append(acc)
         return outs
 
+    def split(values):
+        upper = values.astype(jnp.bfloat16)
+        return upper, (values - upper.astype(jnp.float32)).astype(jnp.bfloat16)
+
+    def product(left, right):
+        return jnp.dot(left, right, preferred_element_type=jnp.float32)
+
     def local(parts):
-        stacked = jnp.concatenate(parts, axis=0)
-        grads = jnp.dot(
-            stacked, forward[...], precision=highest, preferred_element_type=jnp.float32
+        stacked = jnp.concatenate(split(jnp.concatenate(parts, axis=0)), axis=1)
+        ahead = packed[pl.ds(0, LANES), :]
+        ahead_rest = packed[pl.ds(LANES, LANES), :]
+        grads = product(stacked, jnp.concatenate([ahead, ahead], axis=0)) + product(
+            stacked, jnp.concatenate([ahead_rest, ahead_rest], axis=0)
         )
         geom_y = jnp.concatenate([geom[1, :, pl.ds(t * LANES, LANES)] for t in range(tiles)], axis=0)
         geom_z = jnp.concatenate([geom[2, :, pl.ds(t * LANES, LANES)] for t in range(tiles)], axis=0)
         flux = jnp.concatenate([grads[:, :LANES] * geom_y, grads[:, LANES:] * geom_z], axis=1)
-        back = jnp.dot(
-            flux, backward[...], precision=highest, preferred_element_type=jnp.float32
-        )
+        flux, flux_rest = split(flux)
+        behind = packed[pl.ds(2 * LANES, 2 * LANES), :]
+        back = product(flux, behind) + product(flux_rest, behind)
+        back = back[:, :LANES] + back[:, LANES:]
         grad_x = along_x(parts, 0)
         flux_x = [grad_x[t] * geom[0, :, pl.ds(t * LANES, LANES)] for t in range(tiles)]
         back_x = along_x(flux_x, 1)
@@ -278,16 +299,29 @@
         return pltpu.make_async_remote_copy(
             src_ref=outbox.at[step, side],
             dst_ref=inbox.at[step, side ^ 1],
-            send_sem=halo_send.at[step, side],
-            recv_sem=halo_recv.at[step, side ^ 1],
+            send_sem=halo_send.at[0],
+            recv_sem=halo_recv.at[step, side // 2],
             device_id=where_to[side],
             device_id_type=MESH,
         )
 
-    def face_arrival(step, side):
-        return pltpu.make_async_copy(
-            inbox.at[step, side], inbox.at[step, side], halo_recv.at[step, side]
-        )
+    def await_faces(step, axis):
+        low, high = has[2 * axis], has[2 * axis + 1]
+        for count, here in ((2, low & high), (1, low ^ high)):
+
+            @pl.when(here)
+            def _():
+                span = inbox.at[step, pl.ds(2 * axis, count)]
+                pltpu.make_async_copy(span, span, halo_recv.at[step, axis]).wait()
+
+    def await_sent():
+        sides = sum(side.astype(jnp.int32) for side in has)
+        for count in range(1, 5):
+
+            @pl.when(sides == count)
+            def _():
+                span = outbox.at[:, pl.ds(0, count)]
+                pltpu.make_async_copy(span, span, halo_send.at[0]).wait()
 
     def operate(parts, step, ready, beside=lambda: None):
         result = local(parts)
@@ -311,6 +345,9 @@
             outbox[step, 1, pl.ds(ex * EZ, EZ), :] = face_y[pl.ds(ex * EY * EZ + (EY - 1) * EZ, EZ), :]
         send_faces((0, 1))
 
+        if step == 0:
+            make_index()
+
         face_x = jnp.where(low_half, result[0], result[tiles - 1])
         width = EY * EZ
         blank = jnp.zeros((width, LANES), jnp.float32)
@@ -331,14 +368,7 @@
 
         beside()
 
-        def await_faces(sides):
-            for side in sides:
-
-                @pl.when(has[side])
-                def _():
-                    face_arrival(step, side).wait()
-
-        await_faces((0, 1))
+        await_faces(step, 0)
         for ex in range(EX):
             halo_y[pl.ds(ex * EY * EZ, EZ), :] = inbox[step, 0, pl.ds(ex * EZ, EZ), :]
             halo_y[pl.ds(ex * EY * EZ + (EY - 1) * EZ, EZ), :] = inbox[step, 1, pl.ds(ex * EZ, EZ), :]
@@ -348,7 +378,7 @@
             result[t] = result[t] + jnp.where(at_y, take_lanes(in_y, index[t]), 0.0)
             image[:, pl.ds(t * LANES, LANES)] = result[t]
 
-        await_faces((2, 3))
+        await_faces(step, 1)
         halo_z[pl.ds(0, EX * EY, stride=EZ), :] = inbox[step, 2]
         halo_z[pl.ds(EZ - 1, EX * EY, stride=EZ), :] = inbox[step, 3]
         edge_z = row_z == jnp.where(low_half, EZ - 1, 0)
@@ -401,12 +431,13 @@
         return row[:, at : at + 1]
 
     start = None
+    load_coeffs.wait()
     for part in range(4):
         loads[part].wait()
         for at in range(part * chunk, (part + 1) * chunk):
             term = coeffs[at] * basis[at]
             start = term if start is None else start + term
-    for copy in loads[4:]:
+    for copy in load_tables:
         copy.wait()
 
     def greeted():
@@ -481,7 +512,7 @@
         + with_first
     )
     block = jnp.concatenate([gram_part[0] + row] + gram_part[1:], axis=0)
-    sums, _ = all_sum(block, 1, lambda: None)
+    sums, _ = all_sum(block, 1, load_pairs.wait)
     sums = sums / total
     along = sums[0:1]
     norm_one = jnp.sqrt(weight(along, fresh - 1) + epsilon)
@@ -517,13 +548,7 @@
     hess[pl.ds(0, 1), :] = row_first[:, : kept + 2]
     hess[pl.ds(1, 1), :] = row_second[:, : kept + 2]
 
-    for step in range(2):
-        for side in range(4):
-
-            @pl.when(has[side])
-            def _():
-                face_copy(step, side).wait_send()
-
+    await_sent()
     for phase in range(2):
         span = messages[phase][1].at[pl.ds(0, devices - 1)]
         pltpu.make_async_copy(span, span, row_send.at[phase]).wait()
@@ -533,7 +558,7 @@
     kept, elements, points = old_basis.shape
     tiles = points // LANES
     devices = n_wide * n_narrow
-    forward, backward, coef = tables()
+    packed, coef = tables()
     rows, listed = pair_rows(kept)
     pairs = np.zeros((2 * rows, LANES), np.int32)
     for at, (left, right) in enumerate(listed):
@@ -548,22 +573,14 @@
     held = pl.pallas_call(
         functools.partial(kernel, n_wide, n_narrow),
         out_shape=tuple(pltpu.VMEM(shape, f32) for shape in shapes),
-        in_specs=[
-            pl.BlockSpec(memory_space=pltpu.SMEM),
-            anywhere,
-            anywhere,
-            vmem,
-            anywhere,
-            anywhere,
-            anywhere,
-            anywhere,
-        ],
+        in_specs=[anywhere] * 7,
         out_specs=(vmem, vmem),
         scratch_shapes=[
+            pltpu.SMEM(restart_coeffs.shape, f32),
             pltpu.VMEM(old_basis.shape, f32),
             pltpu.VMEM(geometry.shape, f32),
-            pltpu.VMEM(forward.shape, f32),
-            pltpu.VMEM(backward.shape, f32),
+            pltpu.VMEM(orientation.shape, jnp.int32),
+            pltpu.VMEM(packed.shape, jnp.bfloat16),
             pltpu.VMEM(coef.shape, f32),
             pltpu.VMEM((2 * tiles + 1, elements, LANES), jnp.int32),
             pltpu.VMEM((8, LANES), jnp.int32),
@@ -580,15 +597,15 @@
             pltpu.VMEM((devices, 1, LANES), f32),
             pltpu.VMEM((rows, LANES), f32),
             pltpu.VMEM((devices, rows, LANES), f32),
-            pltpu.SemaphoreType.DMA((9,)),
-            pltpu.SemaphoreType.DMA((2, 4)),
-            pltpu.SemaphoreType.DMA((2, 4)),
+            pltpu.SemaphoreType.DMA((10,)),
+            pltpu.SemaphoreType.DMA((1,)),
+            pltpu.SemaphoreType.DMA((2, 2)),
             pltpu.SemaphoreType.DMA((2,)),
             pltpu.SemaphoreType.DMA((2,)),
         ],
         compiler_params=pltpu.CompilerParams(collective_id=0, has_side_effects=True),
         name="arnoldi",
-    )(restart_coeffs, old_basis, geometry, orientation, forward, backward, coef, pairs)
+    )(restart_coeffs, old_basis, geometry, orientation, packed, coef, pairs)
     return held
 
 

time: 27.1 us -> 25.8 us (0.952)
  Pallas kernels: 25 us -> 23.7 us
    pallas_call x1, Pallas kernels: 25 us -> 23.7 us  [on_device(): pl.pallas_call(functools.partial(kernel, n_wide, n_narrow), out_shape=tup...]
where the time goes in v1:
time: 25.8 us; the launch traced here: 25.6 us
  Pallas kernels  23.7 us (92%)
  local copies, waits for them, and re-layouts  1.27 us (5%)
  between operations  0.64 us (2%)
    pallas_call x1, Pallas kernels, on_device(): pl.pallas_call(functools.partial(kernel, n_wide, n_narrow), out_shape=tup...  23.7 us
    unnamed x2, local copies, waits for them, and re-layouts  1.27 us

profile of v1, /device:TPU:0, one launch (start us, length us, event | category | flops | bytes accessed | tf_op | source)
XLA Modules:
  0.0 25.6 jit_solution(348277492452650920)
XLA Ops:
  0.6 23.7 %arnoldi.1 = (f32[2,64,512]{2,1,0:T(8,128)S(1)}, f32[2,18]{1,0:T(2,128)S(1)}) custom-call(f32[16]{0:T(128)} %coeffs_hbm.1, f32[16,64,512]{2,1,0:T(8,128)} %basis_hbm.1, f32[4,64,512]{2,1,0:T(8,128)} %geom_hbm.1, s32[6,64]{1,0:T(8,128)} %orient_hbm.1, bf16[512,256]{1,0:T(8,128)(2,1)} %constant.6.clone.packed_hbm, f32[64,128]{1,0:T(8,128)} %constant.7.clone.coef_hbm, ...), custom_call_target="tpu_custom_call" | custom-call | tf_op jit(solution)/shard_map/arnoldi/pallas_call | solution.py:573
  24.3 0.7 %copy.11 = f32[2,64,512]{2,1,0:T(8,128)} copy(f32[2,64,512]{2,1,0:T(8,128)S(1)} %get-tuple-element.2) | data formatting | bytes 524288
  25.1 0.6 %copy.12 = f32[2,18]{1,0:T(2,128)} copy(f32[2,18]{1,0:T(2,128)S(1)} %get-tuple-element.3) | data formatting | bytes 288

commit v2 on v1

--- a/solution.py
+++ b/solution.py
@@ -138,11 +138,17 @@
     row_in,
     pair_out,
     pair_in,
+    far_code,
+    far_index,
+    far_tile,
+    far_basis,
+    lined,
     load_sem,
     halo_send,
     halo_recv,
     row_send,
     row_recv,
+    all_ready,
 ):
     wide = lax.axis_index("wide")
     narrow = lax.axis_index("narrow")
@@ -198,15 +204,72 @@
 
     barrier = pltpu.get_barrier_semaphore()
 
-    def greet(where):
-        pl.semaphore_signal(barrier, inc=1, device_id=where, device_id_type=MESH)
+    inner = 1
+    while n_wide % (2 * inner) == 0 and 4 * inner * inner <= n_wide:
+        inner = 2 * inner
+    plane = inner * n_narrow
+    planes = n_wide // inner
+    layer = wide // inner
+    column = lax.rem(wide, inner)
+    in_plane = column * n_narrow + narrow
+
+    def in_steps(count, act):
+        if count <= 64:
+            for step in range(count - 1, 0, -1):
+                act(step)
+        else:
+
+            def body(step, carry):
+                act(step)
+                return carry
+
+            lax.fori_loop(1, count, body, 0)
+
+    def signal(semaphore, where):
+        pl.semaphore_signal(semaphore, inc=1, device_id=where, device_id_type=MESH)
+
+    def to_planes(semaphore):
+        def act(step):
+            other = lax.rem(layer + step, planes)
+            signal(semaphore, (other * inner + column, narrow))
+
+        in_steps(planes, act)
+
+    def to_plane(semaphore):
+        def act(step):
+            other = lax.rem(in_plane + step, plane)
+            signal(semaphore, (layer * inner + other // n_narrow, lax.rem(other, n_narrow)))
+
+        in_steps(plane, act)
+
+    greetings = plane + planes - 2
+    crossing = ()
+    if 1 < inner < n_wide:
+        crossing = (
+            ((column == 0) & (wide > 0), -1),
+            ((column == inner - 1) & (wide < n_wide - 1), 1),
+        )
+    for there, shift in crossing:
+        greetings = greetings + there.astype(jnp.int32)
+
+    def greet():
+        to_planes(barrier)
+        for there, shift in crossing:
+
+            @pl.when(there)
+            def _():
+                signal(barrier, (wide + shift, narrow))
+
+        to_plane(barrier)
 
     inbox[...] = jnp.zeros_like(inbox)
-    each_peer(greet)
+    greet()
 
     lane = lax.broadcasted_iota(jnp.int32, (elements, LANES), 1)
     line = lax.broadcasted_iota(jnp.int32, (elements, LANES), 0)
     low_half = lane < FACE
+    border = EX * EY
+    low_border = low_half[:border]
     half = lane // FACE
     mid = (lane // NP) % NP
     fast = lane % NP
@@ -233,6 +296,29 @@
             first_pos = 2 * tile + half
             index[tile] = rotated(first_pos, fast, code_y) + jnp.where(mid == 0, FACE, 0)
             index[tiles + tile] = rotated(first_pos, mid, code_z) + jnp.where(fast == 0, FACE, 0)
+        far_code[...] = jnp.where(low_half, code[5], code[4])
+        found = jnp.where(
+            low_border,
+            far_code[pl.ds(EZ - 1, border, stride=EZ), :],
+            far_code[pl.ds(0, border, stride=EZ), :],
+        )
+        turned = (found & 4) != 0
+        along_a = jnp.where(turned, fast[:border], mid[:border]) ^ (7 * (found & 1))
+        along_b = jnp.where(turned, mid[:border], fast[:border]) ^ (7 * ((found >> 1) & 1))
+        far_index[...] = (along_a % 2) * FACE + along_b * NP + jnp.where(low_border, NP - 1, 0)
+        far_tile[...] = along_a // 2
+
+    def meeting(ref, *at):
+        found = None
+        for t in range(tiles):
+            lanes = pl.ds(t * LANES, LANES)
+            spare = (sum(at) % 2) * tiles + t
+            lined[spare] = ref[at + (slice(None), lanes)]
+            last = lined[spare, pl.ds(EZ - 1, border, stride=EZ), :]
+            begin = lined[spare, pl.ds(0, border, stride=EZ), :]
+            got = take_lanes(jnp.where(fast[:border] == NP - 1, last, begin), far_index[...])
+            found = got if found is None else jnp.where(far_tile[...] == t, got, found)
+        return found
 
     def tile_of(values, tile):
         return values[:, tile * LANES : (tile + 1) * LANES]
@@ -366,6 +452,11 @@
         result[0] = result[0] + jnp.where(low_half, got_x, 0.0)
         result[tiles - 1] = result[tiles - 1] + jnp.where(low_half, 0.0, got_x)
 
+        edge_z = row_z == jnp.where(low_half, EZ - 1, 0)
+        in_z = jnp.where(edge_z, 0.0, in_z)
+        for t in range(tiles):
+            result[t] = result[t] + jnp.where(at_z, take_lanes(in_z, index[tiles + t]), 0.0)
+
         beside()
 
         await_faces(step, 0)
@@ -378,16 +469,21 @@
             result[t] = result[t] + jnp.where(at_y, take_lanes(in_y, index[t]), 0.0)
             image[:, pl.ds(t * LANES, LANES)] = result[t]
 
+    def far_faces(step):
         await_faces(step, 1)
-        halo_z[pl.ds(0, EX * EY, stride=EZ), :] = inbox[step, 2]
-        halo_z[pl.ds(EZ - 1, EX * EY, stride=EZ), :] = inbox[step, 3]
+        return jnp.where(low_border, inbox[step, 3], inbox[step, 2])
+
+    def add_far(step):
+        halo_z[pl.ds(0, border, stride=EZ), :] = inbox[step, 2]
+        halo_z[pl.ds(EZ - 1, border, stride=EZ), :] = inbox[step, 3]
         edge_z = row_z == jnp.where(low_half, EZ - 1, 0)
-        in_z = jnp.where(edge_z, halo_z[...], in_z)
-        return [
-            image[:, pl.ds(t * LANES, LANES)]
-            + jnp.where(at_z, take_lanes(in_z, index[tiles + t]), 0.0)
-            for t in range(tiles)
-        ]
+        in_z = jnp.where(edge_z, halo_z[...], 0.0)
+        for t in range(tiles):
+            got = jnp.where(at_z, take_lanes(in_z, index[tiles + t]), 0.0)
+            image[:, pl.ds(t * LANES, LANES)] = image[:, pl.ds(t * LANES, LANES)] + got
+
+    def stacked_rows(values):
+        return jnp.sum(values.reshape(border // 8, 8, LANES), axis=0)
 
     def folded(values):
         acc = tile_of(values, 0)
@@ -421,6 +517,8 @@
                 device_id_type=MESH,
             ).start()
 
+        if phase == 0:
+            pl.semaphore_wait(all_ready, planes - 1)
         each_peer(send)
         result = beside()
         span = incoming.at[pl.ds(0, devices - 1)]
@@ -441,11 +539,14 @@
         copy.wait()
 
     def greeted():
-        pl.semaphore_wait(barrier, devices - 1)
-
-    image_parts = operate([tile_of(start, t) for t in range(tiles)], 0, greeted)
-    for t in range(tiles):
-        image[:, pl.ds(t * LANES, LANES)] = image_parts[t]
+        pl.semaphore_wait(barrier, greetings)
+        to_planes(all_ready)
+
+    def meet_basis():
+        for at in range(kept):
+            far_basis[at] = meeting(basis, at)
+
+    operate([tile_of(start, t) for t in range(tiles)], 0, greeted, meet_basis)
     rows, listed = pair_rows(kept)
     fresh = 2 * kept + 3
 
@@ -485,8 +586,15 @@
             gram_rows.append(row)
         return gram_rows
 
-    row = to_row([folded(basis[at] * image[...]) for at in range(kept)])
-    sums, gram_part = all_sum(row, 0, gram)
+    near = [folded(basis[at] * image[...]) for at in range(kept)]
+    far = far_faces(0)
+    row = to_row([near[at] + stacked_rows(far_basis[at] * far) for at in range(kept)])
+
+    def between():
+        add_far(0)
+        return gram()
+
+    sums, gram_part = all_sum(row, 0, between)
     proj_one = sums / total
     acc = image[...]
     for at in range(kept):
@@ -496,23 +604,33 @@
     with_first = []
 
     def project_first():
-        with_first.extend(
-            [folded(basis[at] * first[...]) for at in range(kept)]
-            + [folded(first[...] * first[...])]
-        )
-
-    image_parts = operate(
+        with_first.append(meeting(first))
+        with_first.append(
+            to_row(
+                [folded(basis[at] * first[...]) for at in range(kept)]
+                + [folded(first[...] * first[...])],
+                kept + 2,
+            )
+        )
+
+    operate(
         [first[:, pl.ds(t * LANES, LANES)] for t in range(tiles)], 1, lambda: None, project_first
     )
-    for t in range(tiles):
-        image[:, pl.ds(t * LANES, LANES)] = image_parts[t]
-    row = to_row(
-        [folded(basis[at] * image[...]) for at in range(kept)]
-        + [folded(first[...] * image[...]), folded(image[...] * image[...])]
-        + with_first
-    )
-    block = jnp.concatenate([gram_part[0] + row] + gram_part[1:], axis=0)
-    sums, _ = all_sum(block, 1, load_pairs.wait)
+    near = [folded(basis[at] * image[...]) for at in range(kept)]
+    near += [folded(first[...] * image[...]), folded(image[...] * image[...])]
+    far_first, row_first = with_first
+    far_image = 2.0 * meeting(image)
+    far = far_faces(1)
+    beyond = [stacked_rows(far_basis[at] * far) for at in range(kept)]
+    beyond += [stacked_rows(far_first * far), stacked_rows((far_image + far) * far)]
+    row = to_row([one + two for one, two in zip(near, beyond)])
+    block = jnp.concatenate([gram_part[0] + row_first + row] + gram_part[1:], axis=0)
+
+    def before_end():
+        add_far(1)
+        load_pairs.wait()
+
+    sums, _ = all_sum(block, 1, before_end)
     sums = sums / total
     along = sums[0:1]
     norm_one = jnp.sqrt(weight(along, fresh - 1) + epsilon)
@@ -552,6 +670,17 @@
     for phase in range(2):
         span = messages[phase][1].at[pl.ds(0, devices - 1)]
         pltpu.make_async_copy(span, span, row_send.at[phase]).wait()
+
+
+def settle(vectors, matrix, out, hess, sem):
+    copies = [
+        pltpu.make_async_copy(vectors, out, sem.at[0]),
+        pltpu.make_async_copy(matrix, hess, sem.at[1]),
+    ]
+    for copy in copies:
+        copy.start()
+    for copy in copies:
+        copy.wait()
 
 
 def on_device(n_wide, n_narrow, old_basis, restart_coeffs, geometry, orientation):
@@ -597,16 +726,29 @@
             pltpu.VMEM((devices, 1, LANES), f32),
             pltpu.VMEM((rows, LANES), f32),
             pltpu.VMEM((devices, rows, LANES), f32),
+            pltpu.VMEM((elements, LANES), jnp.int32),
+            pltpu.VMEM((border, LANES), jnp.int32),
+            pltpu.VMEM((border, LANES), jnp.int32),
+            pltpu.VMEM((kept, border, LANES), f32),
+            pltpu.VMEM((2 * tiles, elements, LANES), f32),
             pltpu.SemaphoreType.DMA((10,)),
             pltpu.SemaphoreType.DMA((1,)),
             pltpu.SemaphoreType.DMA((2, 2)),
             pltpu.SemaphoreType.DMA((2,)),
             pltpu.SemaphoreType.DMA((2,)),
+            pltpu.SemaphoreType.REGULAR,
         ],
         compiler_params=pltpu.CompilerParams(collective_id=0, has_side_effects=True),
         name="arnoldi",
     )(restart_coeffs, old_basis, geometry, orientation, packed, coef, pairs)
-    return held
+    return pl.pallas_call(
+        settle,
+        out_shape=tuple(jax.ShapeDtypeStruct(shape, f32) for shape in shapes),
+        in_specs=[vmem, vmem],
+        out_specs=(anywhere, anywhere),
+        scratch_shapes=[pltpu.SemaphoreType.DMA((2,))],
+        name="settle",
+    )(*[pltpu.with_memory_space_constraint(each, pltpu.VMEM) for each in held])
 
 
 def solution(mesh):

time: 25.8 us -> 23.3 us (0.903)
  local copies, waits for them, and re-layouts: 1.27 us -> 0 us
  Pallas kernels: 23.7 us -> 22.6 us
    pallas_call x1, Pallas kernels: 23.7 us -> 21.8 us  [on_device(): pl.pallas_call(functools.partial(kernel, n_wide, n_narrow), out_shape=tup...]
    unnamed x2 -> x0, local copies, waits for them, and re-layouts: 1.27 us -> none
    pallas_call x0 -> x1, Pallas kernels: none -> 0.72 us  [on_device(): pl.pallas_call(settle, out_shape=tuple((jax.ShapeDtypeStruct(shape, f32)...]
where the time goes in v2:
time: 23.3 us; the launch traced here: 23.2 us
  Pallas kernels  22.6 us (97%)
  between operations  0.64 us (3%)
    pallas_call x1, Pallas kernels, on_device(): pl.pallas_call(functools.partial(kernel, n_wide, n_narrow), out_shape=tup...  21.8 us
    pallas_call x1, Pallas kernels, on_device(): pl.pallas_call(settle, out_shape=tuple((jax.ShapeDtypeStruct(shape, f32)...  0.72 us

profile of v2, /device:TPU:0, one launch (start us, length us, event | category | flops | bytes accessed | tf_op | source)
XLA Modules:
  0.0 23.2 jit_solution(9851843623114592670)
XLA Ops:
  0.6 21.8 %arnoldi.1 = (f32[2,64,512]{2,1,0:T(8,128)S(1)}, f32[2,18]{1,0:T(2,128)S(1)}) custom-call(f32[16]{0:T(128)} %coeffs_hbm.1, f32[16,64,512]{2,1,0:T(8,128)} %basis_hbm.1, f32[4,64,512]{2,1,0:T(8,128)} %geom_hbm.1, s32[6,64]{1,0:T(8,128)} %orient_hbm.1, bf16[512,256]{1,0:T(8,128)(2,1)} %constant.6.clone.packed_hbm, f32[64,128]{1,0:T(8,128)} %constant.7.clone.coef_hbm, ...), custom_call_target="tpu_custom_call" | custom-call | tf_op jit(solution)/shard_map/arnoldi/pallas_call | solution.py:702
  22.5 0.7 %settle.1 = (f32[2,64,512]{2,1,0:T(8,128)}, f32[2,18]{1,0:T(2,128)}) custom-call(f32[2,64,512]{2,1,0:T(8,128)S(1)} %get-tuple-element.4.vectors, f32[2,18]{1,0:T(2,128)S(1)} %get-tuple-element.5.matrix), custom_call_target="tpu_custom_call" | custom-call | tf_op jit(solution)/shard_map/settle/pallas_call | solution.py:744

commit v3 on v2

--- a/solution.py
+++ b/solution.py
@@ -82,19 +82,6 @@
     )
 
 
-def pair_rows(kept):
-    count = kept + 2
-    listed = [(at, kept + 1) for at in range(count)]
-    listed += [(at, kept) for at in range(kept + 1)]
-    block = 4
-    for left in range(0, kept, block):
-        for right in range(left, kept, block):
-            for one in range(left, left + block):
-                for two in range(max(right, one), right + block):
-                    listed.append((one, two))
-    return -(-len(listed) // LANES), listed
-
-
 def take_lanes(values, index):
     return jnp.take_along_axis(values, index, axis=1, mode="promise_in_bounds")
 
@@ -114,7 +101,6 @@
     orient_hbm,
     packed_hbm,
     coef_hbm,
-    pairs_hbm,
     out,
     hess,
     coeffs,
@@ -133,7 +119,6 @@
     halo_z,
     outbox,
     inbox,
-    pairs,
     row_out,
     row_in,
     pair_out,
@@ -170,11 +155,10 @@
     load_tables = [
         load(packed_hbm, packed, 5),
         load(coef_hbm, coef, 6),
-        load(geom_hbm, geom, 7),
     ]
+    load_geom = load(geom_hbm, geom, 7)
     load_orient = load(orient_hbm, orient, 8)
-    load_pairs = load(pairs_hbm, pairs, 9)
-    for copy in [load_coeffs] + loads + load_tables + [load_orient, load_pairs]:
+    for copy in [load_coeffs] + loads + load_tables + [load_geom, load_orient]:
         copy.start()
 
     messages = ((row_out, row_in), (pair_out, pair_in))
@@ -189,11 +173,8 @@
                     other = other + (1 - 2 * lax.rem(me // 2**bit, 2)) * 2**bit
         return (other // n_narrow, lax.rem(other, n_narrow))
 
-    def each_peer(act):
-        if devices <= 64:
-            for step in range(devices - 1, 0, -1):
-                act(peer(step))
-        else:
+    def each_peer(act, ascending):
+        if devices > 64:
 
             def body(step, carry):
                 other = lax.rem(me + step, devices)
@@ -201,6 +182,13 @@
                 return carry
 
             lax.fori_loop(1, devices, body, 0)
+        elif ascending:
+            for at in range(devices - 1):
+                other = at + (me <= at).astype(jnp.int32)
+                act((other // n_narrow, lax.rem(other, n_narrow)))
+        else:
+            for step in range(devices - 1, 0, -1):
+                act(peer(step))
 
     barrier = pltpu.get_barrier_semaphore()
 
@@ -348,13 +336,15 @@
     def product(left, right):
         return jnp.dot(left, right, preferred_element_type=jnp.float32)
 
-    def local(parts):
+    def local(parts, geometry_here=lambda: None):
         stacked = jnp.concatenate(split(jnp.concatenate(parts, axis=0)), axis=1)
         ahead = packed[pl.ds(0, LANES), :]
         ahead_rest = packed[pl.ds(LANES, LANES), :]
         grads = product(stacked, jnp.concatenate([ahead, ahead], axis=0)) + product(
             stacked, jnp.concatenate([ahead_rest, ahead_rest], axis=0)
         )
+        grad_x = along_x(parts, 0)
+        geometry_here()
         geom_y = jnp.concatenate([geom[1, :, pl.ds(t * LANES, LANES)] for t in range(tiles)], axis=0)
         geom_z = jnp.concatenate([geom[2, :, pl.ds(t * LANES, LANES)] for t in range(tiles)], axis=0)
         flux = jnp.concatenate([grads[:, :LANES] * geom_y, grads[:, LANES:] * geom_z], axis=1)
@@ -362,7 +352,6 @@
         behind = packed[pl.ds(2 * LANES, 2 * LANES), :]
         back = product(flux, behind) + product(flux_rest, behind)
         back = back[:, :LANES] + back[:, LANES:]
-        grad_x = along_x(parts, 0)
         flux_x = [grad_x[t] * geom[0, :, pl.ds(t * LANES, LANES)] for t in range(tiles)]
         back_x = along_x(flux_x, 1)
         return [
@@ -410,7 +399,7 @@
                 pltpu.make_async_copy(span, span, halo_send.at[0]).wait()
 
     def operate(parts, step, ready, beside=lambda: None):
-        result = local(parts)
+        result = local(parts, load_geom.wait if step == 0 else lambda: None)
         def send_faces(sides):
             for side in sides:
 
@@ -491,16 +480,20 @@
             acc = acc + tile_of(values, tile)
         return jnp.sum(acc.reshape(elements // 8, 8, LANES), axis=0)
 
-    def to_row(partials, begin=0):
+    def sums_of(partials):
         count = -(-len(partials) // 8) * 8
         rows = [jnp.sum(part, axis=0, keepdims=True) for part in partials]
         rows += [jnp.zeros((1, LANES), jnp.float32)] * (count - len(rows))
-        block = jnp.concatenate(rows, axis=0)
-        sums = jnp.sum(block, axis=1, keepdims=True)
-        place = lax.broadcasted_iota(jnp.int32, (count, LANES), 0) + begin == lax.broadcasted_iota(
-            jnp.int32, (count, LANES), 1
-        )
-        return jnp.sum(jnp.where(place, sums, 0.0), axis=0, keepdims=True)
+        return jnp.sum(jnp.concatenate(rows, axis=0), axis=1, keepdims=True)
+
+    def put(sums, place_of):
+        shape = (sums.shape[0], LANES)
+        place = place_of(lax.broadcasted_iota(jnp.int32, shape, 0))
+        here = place == lax.broadcasted_iota(jnp.int32, shape, 1)
+        return jnp.sum(jnp.where(here, sums, 0.0), axis=0, keepdims=True)
+
+    def to_row(partials, begin=0):
+        return put(sums_of(partials), lambda at: at + begin)
 
     def all_sum(block, phase, beside):
         outgoing, incoming = messages[phase]
@@ -519,14 +512,49 @@
 
         if phase == 0:
             pl.semaphore_wait(all_ready, planes - 1)
-        each_peer(send)
+        each_peer(send, phase == 1)
         result = beside()
         span = incoming.at[pl.ds(0, devices - 1)]
         pltpu.make_async_copy(span, span, row_recv.at[phase]).wait()
-        return jnp.sum(incoming[...], axis=0), result
+        if devices > 64:
+            return jnp.sum(incoming[...], axis=0), result
+        found = [incoming[at] for at in range(devices)]
+        while len(found) > 1:
+            half_way = len(found) // 2
+            odd = found[2 * half_way :]
+            found = [found[at] + found[half_way + at] for at in range(half_way)] + odd
+        return found[0], result
 
     def weight(row, at):
-        return row[:, at : at + 1]
+        spot = jnp.full((8, LANES), at, jnp.int32)
+        return take_lanes(jnp.broadcast_to(row, (8, LANES)), spot)
+
+    pieces = [
+        (pl.ds(base, 8), pl.ds(tile * LANES, LANES))
+        for base in range(0, elements, 8)
+        for tile in range(tiles)
+    ]
+
+    def against_basis(ref):
+        found = [None] * kept
+        for at in pieces:
+            piece = ref[at]
+            for one in range(kept):
+                term = basis[(one,) + at] * piece
+                found[one] = term if found[one] is None else found[one] + term
+        return found
+
+    def against(left, right):
+        found = None
+        for at in pieces:
+            term = left[at] * right[at]
+            found = term if found is None else found + term
+        return found
+
+    def less_basis(piece, parts, at):
+        for one in range(kept):
+            piece = piece - parts[one] * basis[(one,) + at]
+        return piece
 
     start = None
     load_coeffs.wait()
@@ -547,19 +575,14 @@
             far_basis[at] = meeting(basis, at)
 
     operate([tile_of(start, t) for t in range(tiles)], 0, greeted, meet_basis)
-    rows, listed = pair_rows(kept)
-    fresh = 2 * kept + 3
+    block = 4
+    a_line = LANES // kept
+    lines = kept // a_line
 
     def gram():
-        partials = []
-        block = 4
+        found = [jnp.zeros((1, LANES), jnp.float32)] * lines
         for left in range(0, kept, block):
             for right in range(left, kept, block):
-                wanted = [
-                    (one, two)
-                    for one in range(left, left + block)
-                    for two in range(max(right, one), right + block)
-                ]
 
                 def body(step, carry):
                     base = pl.multiple_of(step * 8, 8)
@@ -570,23 +593,21 @@
                         twos = ones if left == right else [
                             basis[(right + m,) + at] for m in range(block)
                         ]
-                        for spot, (one, two) in enumerate(wanted):
-                            carry[spot] = carry[spot] + ones[one - left] * twos[two - right]
+                        for spot in range(block * block):
+                            carry[spot] = carry[spot] + ones[spot // block] * twos[spot % block]
                     return tuple(carry)
 
                 zero = jnp.zeros((8, LANES), jnp.float32)
-                partials += list(
-                    lax.fori_loop(0, elements // 8, body, (zero,) * len(wanted))
+                partials = lax.fori_loop(0, elements // 8, body, (zero,) * (block * block))
+                begin = (left % a_line) * kept + right
+                row = put(
+                    sums_of(partials), lambda at: begin + (at // block) * kept + at % block
                 )
-        gram_rows = []
-        for begin in range(0, rows * LANES, LANES):
-            lo = max(begin, fresh)
-            here = partials[lo - fresh : begin + LANES - fresh]
-            row = to_row(here, lo - begin) if here else jnp.zeros((1, LANES), jnp.float32)
-            gram_rows.append(row)
-        return gram_rows
-
-    near = [folded(basis[at] * image[...]) for at in range(kept)]
+                line_at = left // a_line
+                found[line_at] = found[line_at] + (row if left == right else 2.0 * row)
+        return found
+
+    near = against_basis(image)
     far = far_faces(0)
     row = to_row([near[at] + stacked_rows(far_basis[at] * far) for at in range(kept)])
 
@@ -594,12 +615,11 @@
         add_far(0)
         return gram()
 
-    sums, gram_part = all_sum(row, 0, between)
+    sums, gram_lines = all_sum(row, 0, between)
     proj_one = sums / total
-    acc = image[...]
-    for at in range(kept):
-        acc = acc - weight(proj_one, at) * basis[at]
-    first[...] = acc
+    parts = [weight(proj_one, at) for at in range(kept)]
+    for at in pieces:
+        first[at] = less_basis(image[at], parts, at)
 
     with_first = []
 
@@ -607,8 +627,7 @@
         with_first.append(meeting(first))
         with_first.append(
             to_row(
-                [folded(basis[at] * first[...]) for at in range(kept)]
-                + [folded(first[...] * first[...])],
+                against_basis(first) + [against(first, first)],
                 kept + 2,
             )
         )
@@ -616,53 +635,61 @@
     operate(
         [first[:, pl.ds(t * LANES, LANES)] for t in range(tiles)], 1, lambda: None, project_first
     )
-    near = [folded(basis[at] * image[...]) for at in range(kept)]
-    near += [folded(first[...] * image[...]), folded(image[...] * image[...])]
+    near = against_basis(image) + [against(first, image), against(image, image)]
     far_first, row_first = with_first
     far_image = 2.0 * meeting(image)
     far = far_faces(1)
     beyond = [stacked_rows(far_basis[at] * far) for at in range(kept)]
     beyond += [stacked_rows(far_first * far), stacked_rows((far_image + far) * far)]
     row = to_row([one + two for one, two in zip(near, beyond)])
-    block = jnp.concatenate([gram_part[0] + row_first + row] + gram_part[1:], axis=0)
-
-    def before_end():
-        add_far(1)
-        load_pairs.wait()
-
-    sums, _ = all_sum(block, 1, before_end)
+    block = jnp.concatenate([row_first + row] + gram_lines, axis=0)
+
+    sums, _ = all_sum(block, 1, lambda: add_far(1))
     sums = sums / total
     along = sums[0:1]
-    norm_one = jnp.sqrt(weight(along, fresh - 1) + epsilon)
+    spot = lax.broadcasted_iota(jnp.int32, (1, LANES), 1)
+    inside = spot < kept
+    parts = [weight(along, at) for at in range(kept)]
+    cross, whole, one = [weight(along, at) for at in (kept, kept + 1, 2 * kept + 2)]
+    with_one = pltpu.roll(jnp.broadcast_to(along, (8, LANES)), LANES - kept - 2, axis=1)[0:1]
+    pick = lax.broadcasted_iota(jnp.int32, (a_line, LANES), 0) * kept + (
+        lax.broadcasted_iota(jnp.int32, (a_line, LANES), 1) % kept
+    )
+    spread = [
+        take_lanes(jnp.broadcast_to(sums[1 + at : 2 + at], (a_line, LANES)), pick)
+        for at in range(lines)
+    ]
+    found = [
+        parts[at][0:1] * spread[at // a_line][at % a_line : at % a_line + 1] for at in range(kept)
+    ]
+    while len(found) > 1:
+        found = [found[at] + found[at + 1] for at in range(0, len(found), 2)]
+    along_in = jnp.where(inside, along, 0.0)
+    terms = jnp.concatenate([along_in * (found[0] - 2.0 * along), along_in * with_one], axis=0)
+    terms = jnp.sum(terms, axis=1, keepdims=True)
+
+    norm_one = jnp.sqrt(one + epsilon)
     scale_one = 1.0 / norm_one
-    proj_two = along * scale_one
-    self_two = weight(along, kept) * scale_one * scale_one
-
-    spot = lax.broadcasted_iota(jnp.int32, (8, LANES), 1)
-    factor = jnp.broadcast_to(along, (8, LANES))
-    factor = jnp.where(spot < kept, -factor, 0.0)
-    factor = jnp.where(spot == kept, -self_two, factor)
-    factor = jnp.where(spot == kept + 1, 1.0, factor)
-    square = jnp.zeros((1, LANES), jnp.float32)
-    for at in range(rows):
-        left = jnp.broadcast_to(pairs[pl.ds(at, 1), :], (8, LANES))
-        right = jnp.broadcast_to(pairs[pl.ds(rows + at, 1), :], (8, LANES))
-        product = take_lanes(factor, left) * take_lanes(factor, right)
-        product = jnp.where(left == right, product, 2.0 * product)
-        used = spot + at * LANES < len(listed)
-        square = square + jnp.where(used, product * sums[at : at + 1], 0.0)[0:1]
-    square = jnp.maximum(jnp.sum(square, axis=1, keepdims=True), 0.0) * (scale_one * scale_one)
+    self_two = cross * (scale_one * scale_one)
+    for at in pieces:
+        piece = first[at]
+        out[(0,) + at] = piece * scale_one
+        image[at] = less_basis(image[at] - self_two * piece, parts, at)
+
+    square = whole + terms[0:1] + self_two * (2.0 * (terms[1:2] - cross) + self_two * one)
+    square = jnp.maximum(square, 0.0) * (scale_one * scale_one)
     norm_two = jnp.sqrt(square + epsilon)
-
-    acc = image[...] - (self_two * first[...])
-    for at in range(kept):
-        acc = acc - weight(along, at) * basis[at]
-    out[0] = first[...] * scale_one
-    out[1] = acc * (scale_one / norm_two)
-
-    spot = lax.broadcasted_iota(jnp.int32, (1, LANES), 1)
-    row_first = jnp.where(spot < kept, proj_one, jnp.where(spot == kept, norm_one, 0.0))
-    row_second = jnp.where(spot < kept, proj_two, jnp.where(spot == kept, self_two, norm_two))
+    scale_two = scale_one / norm_two
+    for at in pieces:
+        out[(1,) + at] = image[at] * scale_two
+
+    norm_one, scale_one, self_two, norm_two = (
+        each[0:1] for each in (norm_one, scale_one, self_two, norm_two)
+    )
+    row_first = jnp.where(inside, proj_one, jnp.where(spot == kept, norm_one, 0.0))
+    row_second = jnp.where(
+        inside, along * scale_one, jnp.where(spot == kept, self_two, norm_two)
+    )
     hess[pl.ds(0, 1), :] = row_first[:, : kept + 2]
     hess[pl.ds(1, 1), :] = row_second[:, : kept + 2]
 
@@ -688,12 +715,7 @@
     tiles = points // LANES
     devices = n_wide * n_narrow
     packed, coef = tables()
-    rows, listed = pair_rows(kept)
-    pairs = np.zeros((2 * rows, LANES), np.int32)
-    for at, (left, right) in enumerate(listed):
-        pairs[at // LANES, at % LANES] = left
-        pairs[rows + at // LANES, at % LANES] = right
-    pairs = jnp.asarray(pairs)
+    rows = 1 + kept * kept // LANES
     anywhere = pl.BlockSpec(memory_space=pl.ANY)
     vmem = pl.BlockSpec(memory_space=pltpu.VMEM)
     f32 = jnp.float32
@@ -702,7 +724,7 @@
     held = pl.pallas_call(
         functools.partial(kernel, n_wide, n_narrow),
         out_shape=tuple(pltpu.VMEM(shape, f32) for shape in shapes),
-        in_specs=[anywhere] * 7,
+        in_specs=[anywhere] * 6,
         out_specs=(vmem, vmem),
         scratch_shapes=[
             pltpu.SMEM(restart_coeffs.shape, f32),
@@ -721,7 +743,6 @@
             pltpu.VMEM((elements, LANES), f32),
             pltpu.VMEM((2, 4, border, LANES), f32),
             pltpu.VMEM((2, 4, border, LANES), f32),
-            pltpu.VMEM(pairs.shape, jnp.int32),
             pltpu.VMEM((1, LANES), f32),
             pltpu.VMEM((devices, 1, LANES), f32),
             pltpu.VMEM((rows, LANES), f32),
@@ -731,7 +752,7 @@
             pltpu.VMEM((border, LANES), jnp.int32),
             pltpu.VMEM((kept, border, LANES), f32),
             pltpu.VMEM((2 * tiles, elements, LANES), f32),
-            pltpu.SemaphoreType.DMA((10,)),
+            pltpu.SemaphoreType.DMA((9,)),
             pltpu.SemaphoreType.DMA((1,)),
             pltpu.SemaphoreType.DMA((2, 2)),
             pltpu.SemaphoreType.DMA((2,)),
@@ -740,7 +761,7 @@
         ],
         compiler_params=pltpu.CompilerParams(collective_id=0, has_side_effects=True),
         name="arnoldi",
-    )(restart_coeffs, old_basis, geometry, orientation, packed, coef, pairs)
+    )(restart_coeffs, old_basis, geometry, orientation, packed, coef)
     return pl.pallas_call(
         settle,
         out_shape=tuple(jax.ShapeDtypeStruct(shape, f32) for shape in shapes),

time: 23.3 us -> 23 us (0.987)
  Pallas kernels: 22.6 us -> 22.2 us
    pallas_call x1, Pallas kernels: 21.8 us -> 21.5 us  [on_device(): pl.pallas_call(functools.partial(kernel, n_wide, n_narrow), out_shape=tup...]
where the time goes in v3:
time: 23 us; the launch traced here: 22.8 us
  Pallas kernels  22.2 us (97%)
  between operations  0.64 us (3%)
    pallas_call x1, Pallas kernels, on_device(): pl.pallas_call(functools.partial(kernel, n_wide, n_narrow), out_shape=tup...  21.5 us
    pallas_call x1, Pallas kernels, on_device(): pl.pallas_call(settle, out_shape=tuple((jax.ShapeDtypeStruct(shape, f32)...  0.72 us

profile of v3, /device:TPU:0, one launch (start us, length us, event | category | flops | bytes accessed | tf_op | source)
XLA Modules:
  0.0 22.8 jit_solution(12437193111324138230)
XLA Ops:
  0.6 21.5 %arnoldi.1 = (f32[2,64,512]{2,1,0:T(8,128)S(1)}, f32[2,18]{1,0:T(2,128)S(1)}) custom-call(f32[16]{0:T(128)} %coeffs_hbm.1, f32[16,64,512]{2,1,0:T(8,128)} %basis_hbm.1, f32[4,64,512]{2,1,0:T(8,128)} %geom_hbm.1, s32[6,64]{1,0:T(8,128)} %orient_hbm.1, bf16[512,256]{1,0:T(8,128)(2,1)} %constant.4.clone.packed_hbm, f32[64,128]{1,0:T(8,128)} %constant.5.clone.coef_hbm), custom_call_target="tpu_custom_call" | custom-call | tf_op jit(solution)/shard_map/arnoldi/pallas_call | solution.py:724
  22.1 0.7 %settle.1 = (f32[2,64,512]{2,1,0:T(8,128)}, f32[2,18]{1,0:T(2,128)}) custom-call(f32[2,64,512]{2,1,0:T(8,128)S(1)} %get-tuple-element.4.vectors, f32[2,18]{1,0:T(2,128)S(1)} %get-tuple-element.5.matrix), custom_call_target="tpu_custom_call" | custom-call | tf_op jit(solution)/shard_map/settle/pallas_call | solution.py:765

commit v4 on v3

--- a/solution.py
+++ b/solution.py
@@ -82,6 +82,14 @@
     )
 
 
+def places():
+    order = [0, EZ - 1] + list(range(1, EZ - 1))
+    width = EX * EY
+    return [
+        (slot * width + at, at * EZ + layer) for slot, layer in enumerate(order) for at in range(width)
+    ]
+
+
 def take_lanes(values, index):
     return jnp.take_along_axis(values, index, axis=1, mode="promise_in_bounds")
 
@@ -114,26 +122,21 @@
     image,
     first,
     face_y,
-    face_z,
     halo_y,
-    halo_z,
     outbox,
     inbox,
     row_out,
     row_in,
     pair_out,
     pair_in,
-    far_code,
     far_index,
     far_tile,
     far_basis,
-    lined,
     load_sem,
-    halo_send,
     halo_recv,
-    row_send,
     row_recv,
     all_ready,
+    from_below,
 ):
     wide = lax.axis_index("wide")
     narrow = lax.axis_index("narrow")
@@ -146,21 +149,29 @@
     def load(source, target, slot):
         return pltpu.make_async_copy(source, target, load_sem.at[slot])
 
-    chunk = kept // 4
-    loads = [
-        load(basis_hbm.at[pl.ds(part * chunk, chunk)], basis.at[pl.ds(part * chunk, chunk)], part)
-        for part in range(4)
-    ]
-    load_coeffs = load(coeffs_hbm, coeffs, 4)
-    load_tables = [
-        load(packed_hbm, packed, 5),
-        load(coef_hbm, coef, 6),
-    ]
-    load_geom = load(geom_hbm, geom, 7)
-    load_orient = load(orient_hbm, orient, 8)
-    for copy in [load_coeffs] + loads + load_tables + [load_geom, load_orient]:
+    width = EX * EY
+    edge = 2 * width
+
+    def load_rows(source, target, begin, count, slot):
+        copies = [
+            load(source.at[:, pl.ds(there, 1)], target.at[:, pl.ds(here, 1)], slot)
+            for here, there in places()[begin : begin + count]
+        ]
+        for copy in copies:
+            copy.start()
+
+    def await_rows(target, begin, count, slot):
+        span = target.at[:, pl.ds(begin, count)]
+        load(span, span, slot).wait()
+
+    load_coeffs = load(coeffs_hbm, coeffs, 6)
+    load_tables = [load(packed_hbm, packed, 7), load(coef_hbm, coef, 8)]
+    load_orient = load(orient_hbm, orient, 9)
+    load_coeffs.start()
+    for copy in load_tables:
         copy.start()
-
+    for slot in range(2):
+        load_rows(basis_hbm, basis, slot * width, width, slot)
     messages = ((row_out, row_in), (pair_out, pair_in))
 
     def peer(step):
@@ -216,12 +227,18 @@
     def signal(semaphore, where):
         pl.semaphore_signal(semaphore, inc=1, device_id=where, device_id_type=MESH)
 
-    def to_planes(semaphore):
-        def act(step):
-            other = lax.rem(layer + step, planes)
+    def to_layer(semaphore, other, there):
+        @pl.when(there)
+        def _():
             signal(semaphore, (other * inner + column, narrow))
 
-        in_steps(planes, act)
+    def to_higher(semaphore):
+        for step in range(planes - 1, 0, -1):
+            to_layer(semaphore, layer + step, layer + step < planes)
+
+    def to_lower(semaphore):
+        for step in range(planes - 1, 0, -1):
+            to_layer(semaphore, layer - step, layer >= step)
 
     def to_plane(semaphore):
         def act(step):
@@ -230,7 +247,9 @@
 
         in_steps(plane, act)
 
-    greetings = plane + planes - 2
+    below = layer > 0
+    above = layer < planes - 1
+    greetings = plane - 1 + layer + above.astype(jnp.int32)
     crossing = ()
     if 1 < inner < n_wide:
         crossing = (
@@ -241,7 +260,8 @@
         greetings = greetings + there.astype(jnp.int32)
 
     def greet():
-        to_planes(barrier)
+        to_layer(barrier, layer - 1, below)
+        to_higher(barrier)
         for there, shift in crossing:
 
             @pl.when(there)
@@ -252,17 +272,22 @@
 
     inbox[...] = jnp.zeros_like(inbox)
     greet()
+    load_rows(geom_hbm, geom, 0, edge, 4)
+    for slot in range(2, EZ):
+        load_rows(basis_hbm, basis, slot * width, width, slot)
+    load_rows(geom_hbm, geom, edge, elements - edge, 5)
+    load_orient.start()
 
     lane = lax.broadcasted_iota(jnp.int32, (elements, LANES), 1)
     line = lax.broadcasted_iota(jnp.int32, (elements, LANES), 0)
     low_half = lane < FACE
-    border = EX * EY
+    border = width
     low_border = low_half[:border]
     half = lane // FACE
     mid = (lane // NP) % NP
     fast = lane % NP
-    row_y = (line // EZ) % EY
-    row_z = line % EZ
+    row_x = (line // EY) % EX
+    row_y = line % EY
     at_y = (mid == 0) | (mid == NP - 1)
     at_z = (fast == 0) | (fast == NP - 1)
 
@@ -274,7 +299,11 @@
         load_orient.wait()
         orient_pad[...] = jnp.zeros_like(orient_pad)
         orient_pad[pl.ds(0, 6), pl.ds(0, elements)] = orient[...]
-        codes = jnp.transpose(orient_pad[...])[:elements]
+        across = lax.broadcasted_iota(jnp.int32, (8, LANES), 1)
+        slot = (across // width) % EZ
+        depth = jnp.where(slot < 2, slot * (EZ - 1), slot - 1)
+        shuffled = take_lanes(orient_pad[...], (across % width) * EZ + depth)
+        codes = jnp.transpose(shuffled)[:elements]
         code = [jnp.broadcast_to(codes[:, f : f + 1], (elements, LANES)) for f in range(6)]
         code_x = jnp.where(low_half, code[0], code[1])
         index[2 * tiles] = rotated(mid, fast, code_x) + jnp.where(low_half, FACE, 0)
@@ -284,12 +313,7 @@
             first_pos = 2 * tile + half
             index[tile] = rotated(first_pos, fast, code_y) + jnp.where(mid == 0, FACE, 0)
             index[tiles + tile] = rotated(first_pos, mid, code_z) + jnp.where(fast == 0, FACE, 0)
-        far_code[...] = jnp.where(low_half, code[5], code[4])
-        found = jnp.where(
-            low_border,
-            far_code[pl.ds(EZ - 1, border, stride=EZ), :],
-            far_code[pl.ds(0, border, stride=EZ), :],
-        )
+        found = jnp.where(low_border, code[5][width:edge], code[4][:width])
         turned = (found & 4) != 0
         along_a = jnp.where(turned, fast[:border], mid[:border]) ^ (7 * (found & 1))
         along_b = jnp.where(turned, mid[:border], fast[:border]) ^ (7 * ((found >> 1) & 1))
@@ -300,10 +324,8 @@
         found = None
         for t in range(tiles):
             lanes = pl.ds(t * LANES, LANES)
-            spare = (sum(at) % 2) * tiles + t
-            lined[spare] = ref[at + (slice(None), lanes)]
-            last = lined[spare, pl.ds(EZ - 1, border, stride=EZ), :]
-            begin = lined[spare, pl.ds(0, border, stride=EZ), :]
+            last = ref[at + (pl.ds(width, width), lanes)]
+            begin = ref[at + (pl.ds(0, width), lanes)]
             got = take_lanes(jnp.where(fast[:border] == NP - 1, last, begin), far_index[...])
             found = got if found is None else jnp.where(far_tile[...] == t, got, found)
         return found
@@ -336,7 +358,8 @@
     def product(left, right):
         return jnp.dot(left, right, preferred_element_type=jnp.float32)
 
-    def local(parts, geometry_here=lambda: None):
+    def local(parts, rows, geometry_here=lambda: None):
+        count = parts[0].shape[0]
         stacked = jnp.concatenate(split(jnp.concatenate(parts, axis=0)), axis=1)
         ahead = packed[pl.ds(0, LANES), :]
         ahead_rest = packed[pl.ds(LANES, LANES), :]
@@ -345,26 +368,28 @@
         )
         grad_x = along_x(parts, 0)
         geometry_here()
-        geom_y = jnp.concatenate([geom[1, :, pl.ds(t * LANES, LANES)] for t in range(tiles)], axis=0)
-        geom_z = jnp.concatenate([geom[2, :, pl.ds(t * LANES, LANES)] for t in range(tiles)], axis=0)
+        geom_y = jnp.concatenate([geom[1, rows, pl.ds(t * LANES, LANES)] for t in range(tiles)], axis=0)
+        geom_z = jnp.concatenate([geom[2, rows, pl.ds(t * LANES, LANES)] for t in range(tiles)], axis=0)
         flux = jnp.concatenate([grads[:, :LANES] * geom_y, grads[:, LANES:] * geom_z], axis=1)
         flux, flux_rest = split(flux)
         behind = packed[pl.ds(2 * LANES, 2 * LANES), :]
         back = product(flux, behind) + product(flux_rest, behind)
         back = back[:, :LANES] + back[:, LANES:]
-        flux_x = [grad_x[t] * geom[0, :, pl.ds(t * LANES, LANES)] for t in range(tiles)]
+        flux_x = [grad_x[t] * geom[0, rows, pl.ds(t * LANES, LANES)] for t in range(tiles)]
         back_x = along_x(flux_x, 1)
         return [
-            back[t * elements : (t + 1) * elements]
+            back[t * count : (t + 1) * count]
             + back_x[t]
-            + geom[3, :, pl.ds(t * LANES, LANES)] * parts[t]
+            + geom[3, rows, pl.ds(t * LANES, LANES)] * parts[t]
             for t in range(tiles)
         ]
 
     def faces(parts, pick):
+        count = parts[0].shape[0]
+        pick, source = pick[:count], source_tile[:count]
         found = take_lanes(parts[0], pick)
         for tile in range(1, tiles):
-            found = jnp.where(source_tile == tile, take_lanes(parts[tile], pick), found)
+            found = jnp.where(source == tile, take_lanes(parts[tile], pick), found)
         return found
 
     has = (narrow > 0, narrow < n_narrow - 1, wide > 0, wide < n_wide - 1)
@@ -372,10 +397,10 @@
 
     def face_copy(step, side):
         return pltpu.make_async_remote_copy(
-            src_ref=outbox.at[step, side],
+            src_ref=outbox.at[step, min(side, 2)],
             dst_ref=inbox.at[step, side ^ 1],
-            send_sem=halo_send.at[0],
-            recv_sem=halo_recv.at[step, side // 2],
+            send_sem=load_sem.at[6],
+            recv_sem=halo_recv.at[side // 2],
             device_id=where_to[side],
             device_id_type=MESH,
         )
@@ -387,7 +412,7 @@
             @pl.when(here)
             def _():
                 span = inbox.at[step, pl.ds(2 * axis, count)]
-                pltpu.make_async_copy(span, span, halo_recv.at[step, axis]).wait()
+                pltpu.make_async_copy(span, span, halo_recv.at[axis]).wait()
 
     def await_sent():
         sides = sum(side.astype(jnp.int32) for side in has)
@@ -395,11 +420,12 @@
 
             @pl.when(sides == count)
             def _():
-                span = outbox.at[:, pl.ds(0, count)]
-                pltpu.make_async_copy(span, span, halo_send.at[0]).wait()
-
-    def operate(parts, step, ready, beside=lambda: None):
-        result = local(parts, load_geom.wait if step == 0 else lambda: None)
+                span = inbox.at[:, pl.ds(0, count)]
+                pltpu.make_async_copy(span, span, load_sem.at[6]).wait()
+
+    ahead_of_most = 2 * layer < planes
+
+    def operate(prepare, step, ready, beside):
         def send_faces(sides):
             for side in sides:
 
@@ -407,51 +433,84 @@
                 def _():
                     face_copy(step, side).start()
 
-        found_z = faces(result, pick_z)
-        face_z[...] = found_z
-        outbox[step, 2] = face_z[pl.ds(0, EX * EY, stride=EZ), :]
-        outbox[step, 3] = face_z[pl.ds(EZ - 1, EX * EY, stride=EZ), :]
-        ready()
-        send_faces((2, 3))
+        parts = prepare(0)
+        rows = pl.ds(0, edge)
+        outer = local(parts, rows, lambda: step or await_rows(geom, 0, edge, 4))
+        ends = [
+            jnp.where(fast[:width] == NP - 1, part[width:], part[:width]) for part in outer
+        ]
+        outbox[step, 2] = faces(ends, pick_z)
+
+        def inner_work():
+            parts = prepare(1)
+            rows = pl.ds(edge, elements - edge)
+            found = local(
+                parts, rows, lambda: step or await_rows(geom, edge, elements - edge, 5)
+            )
+            if step == 0:
+                for t in range(tiles):
+                    image[rows, pl.ds(t * LANES, LANES)] = found[t]
+                return None
+            return found
+
+        if step == 0:
+            pl.when(ahead_of_most)(inner_work)
+            ready()
+            send_faces((2, 3))
+            pl.when(jnp.logical_not(ahead_of_most))(inner_work)
+            inner_part = [
+                image[pl.ds(edge, elements - edge), pl.ds(t * LANES, LANES)] for t in range(tiles)
+            ]
+        else:
+            send_faces((2, 3))
+            inner_part = inner_work()
+        result = [jnp.concatenate(pair, axis=0) for pair in zip(outer, inner_part)]
         found_y = faces(result, pick_y)
         face_y[...] = found_y
-        for ex in range(EX):
-            outbox[step, 0, pl.ds(ex * EZ, EZ), :] = face_y[pl.ds(ex * EY * EZ, EZ), :]
-            outbox[step, 1, pl.ds(ex * EZ, EZ), :] = face_y[pl.ds(ex * EY * EZ + (EY - 1) * EZ, EZ), :]
+        outbox[step, 0] = face_y[pl.ds(0, width, stride=EY), :]
+        outbox[step, 1] = face_y[pl.ds(EY - 1, width, stride=EY), :]
         send_faces((0, 1))
+        found_z = faces(result, pick_z)
 
         if step == 0:
             make_index()
 
         face_x = jnp.where(low_half, result[0], result[tiles - 1])
-        width = EY * EZ
-        blank = jnp.zeros((width, LANES), jnp.float32)
         in_x = jnp.where(
             low_half,
-            jnp.concatenate([face_x[width:], blank], axis=0),
-            jnp.concatenate([blank, face_x[: elements - width]], axis=0),
+            jnp.where(row_x < EX - 1, pltpu.roll(face_x, elements - EY, axis=0), 0.0),
+            jnp.where(row_x > 0, pltpu.roll(face_x, EY, axis=0), 0.0),
         )
         in_y = jnp.where(
-            low_half, pltpu.roll(found_y, elements - EZ, axis=0), pltpu.roll(found_y, EZ, axis=0)
-        )
-        in_z = jnp.where(
-            low_half, pltpu.roll(found_z, elements - 1, axis=0), pltpu.roll(found_z, 1, axis=0)
+            low_half, pltpu.roll(found_y, elements - 1, axis=0), pltpu.roll(found_y, 1, axis=0)
+        )
+        slot_of = [0] + list(range(2, EZ)) + [1]
+        blank = jnp.zeros((width, LANES), jnp.float32)
+
+        def layer(at):
+            if at < 0 or at >= EZ:
+                return blank
+            return found_z[slot_of[at] * width : (slot_of[at] + 1) * width]
+
+        in_z = jnp.concatenate(
+            [
+                jnp.where(low_border, layer(at + 1), layer(at - 1))
+                for at in [0, EZ - 1] + list(range(1, EZ - 1))
+            ],
+            axis=0,
         )
         got_x = take_lanes(in_x, index[2 * tiles])
         result[0] = result[0] + jnp.where(low_half, got_x, 0.0)
         result[tiles - 1] = result[tiles - 1] + jnp.where(low_half, 0.0, got_x)
 
-        edge_z = row_z == jnp.where(low_half, EZ - 1, 0)
-        in_z = jnp.where(edge_z, 0.0, in_z)
         for t in range(tiles):
             result[t] = result[t] + jnp.where(at_z, take_lanes(in_z, index[tiles + t]), 0.0)
 
         beside()
 
         await_faces(step, 0)
-        for ex in range(EX):
-            halo_y[pl.ds(ex * EY * EZ, EZ), :] = inbox[step, 0, pl.ds(ex * EZ, EZ), :]
-            halo_y[pl.ds(ex * EY * EZ + (EY - 1) * EZ, EZ), :] = inbox[step, 1, pl.ds(ex * EZ, EZ), :]
+        halo_y[pl.ds(0, width, stride=EY), :] = inbox[step, 0]
+        halo_y[pl.ds(EY - 1, width, stride=EY), :] = inbox[step, 1]
         edge_y = row_y == jnp.where(low_half, EY - 1, 0)
         in_y = jnp.where(edge_y, halo_y[...], in_y)
         for t in range(tiles):
@@ -463,13 +522,17 @@
         return jnp.where(low_border, inbox[step, 3], inbox[step, 2])
 
     def add_far(step):
-        halo_z[pl.ds(0, border, stride=EZ), :] = inbox[step, 2]
-        halo_z[pl.ds(EZ - 1, border, stride=EZ), :] = inbox[step, 3]
-        edge_z = row_z == jnp.where(low_half, EZ - 1, 0)
-        in_z = jnp.where(edge_z, halo_z[...], 0.0)
+        in_z = jnp.concatenate(
+            [
+                jnp.where(low_border, 0.0, inbox[step, 2]),
+                jnp.where(low_border, inbox[step, 3], 0.0),
+            ],
+            axis=0,
+        )
         for t in range(tiles):
-            got = jnp.where(at_z, take_lanes(in_z, index[tiles + t]), 0.0)
-            image[:, pl.ds(t * LANES, LANES)] = image[:, pl.ds(t * LANES, LANES)] + got
+            at = (pl.ds(0, edge), pl.ds(t * LANES, LANES))
+            got = take_lanes(in_z, index[tiles + t, pl.ds(0, edge), :])
+            image[at] = image[at] + jnp.where(at_z[:edge], got, 0.0)
 
     def stacked_rows(values):
         return jnp.sum(values.reshape(border // 8, 8, LANES), axis=0)
@@ -504,18 +567,26 @@
             pltpu.make_async_remote_copy(
                 src_ref=outgoing,
                 dst_ref=incoming.at[me],
-                send_sem=row_send.at[phase],
-                recv_sem=row_recv.at[phase],
+                send_sem=load_sem.at[7 + phase],
+                recv_sem=(row_recv if phase == 0 else load_sem).at[0],
                 device_id=where,
                 device_id_type=MESH,
             ).start()
 
         if phase == 0:
-            pl.semaphore_wait(all_ready, planes - 1)
+
+            @pl.when(above)
+            def _():
+                pl.semaphore_wait(all_ready, planes - 1 - layer)
+
+            @pl.when(below & jnp.logical_not(above))
+            def _():
+                pl.semaphore_wait(from_below, 1)
+
         each_peer(send, phase == 1)
         result = beside()
         span = incoming.at[pl.ds(0, devices - 1)]
-        pltpu.make_async_copy(span, span, row_recv.at[phase]).wait()
+        pltpu.make_async_copy(span, span, (row_recv if phase == 0 else load_sem).at[0]).wait()
         if devices > 64:
             return jnp.sum(incoming[...], axis=0), result
         found = [incoming[at] for at in range(devices)]
@@ -551,30 +622,53 @@
             found = term if found is None else found + term
         return found
 
+    def store_out(which, at, piece):
+        begin, tile = at[0].start, at[1].start // LANES
+        out[which, tile, pl.ds(places()[begin][1], 8, stride=EZ), :] = piece
+
     def less_basis(piece, parts, at):
         for one in range(kept):
             piece = piece - parts[one] * basis[(one,) + at]
         return piece
 
-    start = None
     load_coeffs.wait()
-    for part in range(4):
-        loads[part].wait()
-        for at in range(part * chunk, (part + 1) * chunk):
-            term = coeffs[at] * basis[at]
-            start = term if start is None else start + term
-    for copy in load_tables:
-        copy.wait()
+
+    def start_of(half):
+        slots = (0, 1) if half == 0 else range(2, EZ)
+        parts = [[] for t in range(tiles)]
+        for slot in slots:
+            await_rows(basis, slot * width, width, slot)
+            for base in range(slot * width, (slot + 1) * width, 8):
+                for t in range(tiles):
+                    at = (pl.ds(base, 8), pl.ds(t * LANES, LANES))
+                    found = None
+                    for one in range(kept):
+                        term = coeffs[one] * basis[(one,) + at]
+                        found = term if found is None else found + term
+                    parts[t].append(found)
+        if half == 0:
+            for copy in load_tables:
+                copy.wait()
+        return [jnp.concatenate(part, axis=0) for part in parts]
 
     def greeted():
         pl.semaphore_wait(barrier, greetings)
-        to_planes(all_ready)
+        to_lower(all_ready)
+        to_layer(from_below, layer + 1, jnp.logical_not(below) & above)
+
+    def relay():
+        @pl.when(below & above)
+        def _():
+            pl.semaphore_wait(from_below, 1)
+
+        to_layer(from_below, layer + 1, below & above)
 
     def meet_basis():
+        relay()
         for at in range(kept):
             far_basis[at] = meeting(basis, at)
 
-    operate([tile_of(start, t) for t in range(tiles)], 0, greeted, meet_basis)
+    operate(start_of, 0, greeted, meet_basis)
     block = 4
     a_line = LANES // kept
     lines = kept // a_line
@@ -618,8 +712,16 @@
     sums, gram_lines = all_sum(row, 0, between)
     proj_one = sums / total
     parts = [weight(proj_one, at) for at in range(kept)]
-    for at in pieces:
-        first[at] = less_basis(image[at], parts, at)
+    def first_of(half):
+        begin, end = (0, edge) if half == 0 else (edge, elements)
+        found = []
+        for t in range(tiles):
+            lanes = pl.ds(t * LANES, LANES)
+            for base in range(begin, end, 8):
+                at = (pl.ds(base, 8), lanes)
+                first[at] = less_basis(image[at], parts, at)
+            found.append(first[pl.ds(begin, end - begin), lanes])
+        return found
 
     with_first = []
 
@@ -632,9 +734,7 @@
             )
         )
 
-    operate(
-        [first[:, pl.ds(t * LANES, LANES)] for t in range(tiles)], 1, lambda: None, project_first
-    )
+    operate(first_of, 1, lambda: None, project_first)
     near = against_basis(image) + [against(first, image), against(image, image)]
     far_first, row_first = with_first
     far_image = 2.0 * meeting(image)
@@ -673,7 +773,7 @@
     self_two = cross * (scale_one * scale_one)
     for at in pieces:
         piece = first[at]
-        out[(0,) + at] = piece * scale_one
+        store_out(0, at, piece * scale_one)
         image[at] = less_basis(image[at] - self_two * piece, parts, at)
 
     square = whole + terms[0:1] + self_two * (2.0 * (terms[1:2] - cross) + self_two * one)
@@ -681,7 +781,7 @@
     norm_two = jnp.sqrt(square + epsilon)
     scale_two = scale_one / norm_two
     for at in pieces:
-        out[(1,) + at] = image[at] * scale_two
+        store_out(1, at, image[at] * scale_two)
 
     norm_one, scale_one, self_two, norm_two = (
         each[0:1] for each in (norm_one, scale_one, self_two, norm_two)
@@ -696,18 +796,21 @@
     await_sent()
     for phase in range(2):
         span = messages[phase][1].at[pl.ds(0, devices - 1)]
-        pltpu.make_async_copy(span, span, row_send.at[phase]).wait()
+        pltpu.make_async_copy(span, span, load_sem.at[7 + phase]).wait()
 
 
 def settle(vectors, matrix, out, hess, sem):
-    copies = [
-        pltpu.make_async_copy(vectors, out, sem.at[0]),
-        pltpu.make_async_copy(matrix, hess, sem.at[1]),
-    ]
+    copies = [pltpu.make_async_copy(matrix, hess, sem.at[1])]
+    tiles = vectors.shape[1]
+    for tile in range(tiles):
+        lanes = pl.ds(tile * LANES, LANES)
+        copies.append(
+            pltpu.make_async_copy(vectors.at[:, tile], out.at[:, :, lanes], sem.at[0])
+        )
     for copy in copies:
         copy.start()
-    for copy in copies:
-        copy.wait()
+    pltpu.make_async_copy(out, out, sem.at[0]).wait()
+    copies[0].wait()
 
 
 def on_device(n_wide, n_narrow, old_basis, restart_coeffs, geometry, orientation):
@@ -720,7 +823,7 @@
     vmem = pl.BlockSpec(memory_space=pltpu.VMEM)
     f32 = jnp.float32
     border = EX * EY
-    shapes = ((2, elements, points), (2, kept + 2))
+    shapes = ((2, tiles, elements, LANES), (2, kept + 2))
     held = pl.pallas_call(
         functools.partial(kernel, n_wide, n_narrow),
         out_shape=tuple(pltpu.VMEM(shape, f32) for shape in shapes),
@@ -739,24 +842,19 @@
             pltpu.VMEM((elements, points), f32),
             pltpu.VMEM((elements, LANES), f32),
             pltpu.VMEM((elements, LANES), f32),
-            pltpu.VMEM((elements, LANES), f32),
-            pltpu.VMEM((elements, LANES), f32),
-            pltpu.VMEM((2, 4, border, LANES), f32),
+            pltpu.VMEM((2, 3, border, LANES), f32),
             pltpu.VMEM((2, 4, border, LANES), f32),
             pltpu.VMEM((1, LANES), f32),
             pltpu.VMEM((devices, 1, LANES), f32),
             pltpu.VMEM((rows, LANES), f32),
             pltpu.VMEM((devices, rows, LANES), f32),
-            pltpu.VMEM((elements, LANES), jnp.int32),
             pltpu.VMEM((border, LANES), jnp.int32),
             pltpu.VMEM((border, LANES), jnp.int32),
             pltpu.VMEM((kept, border, LANES), f32),
-            pltpu.VMEM((2 * tiles, elements, LANES), f32),
-            pltpu.SemaphoreType.DMA((9,)),
+            pltpu.SemaphoreType.DMA((10,)),
+            pltpu.SemaphoreType.DMA((2,)),
             pltpu.SemaphoreType.DMA((1,)),
-            pltpu.SemaphoreType.DMA((2, 2)),
-            pltpu.SemaphoreType.DMA((2,)),
-            pltpu.SemaphoreType.DMA((2,)),
+            pltpu.SemaphoreType.REGULAR,
             pltpu.SemaphoreType.REGULAR,
         ],
         compiler_params=pltpu.CompilerParams(collective_id=0, has_side_effects=True),
@@ -764,7 +862,9 @@
     )(restart_coeffs, old_basis, geometry, orientation, packed, coef)
     return pl.pallas_call(
         settle,
-        out_shape=tuple(jax.ShapeDtypeStruct(shape, f32) for shape in shapes),
+        out_shape=tuple(
+            jax.ShapeDtypeStruct(shape, f32) for shape in ((2, elements, points), shapes[1])
+        ),
         in_specs=[vmem, vmem],
         out_specs=(anywhere, anywhere),
         scratch_shapes=[pltpu.SemaphoreType.DMA((2,))],

time: 23 us -> 22.6 us (0.983)
  Pallas kernels: 22.2 us -> 21.8 us
    pallas_call x1, Pallas kernels: 21.5 us -> 21 us  [on_device(): pl.pallas_call(functools.partial(kernel, n_wide, n_narrow), out_shape=tup...]
where the time goes in v4:
time: 22.6 us; the launch traced here: 22.4 us
  Pallas kernels  21.8 us (96%)
  between operations  0.64 us (3%)
    pallas_call x1, Pallas kernels, on_device(): pl.pallas_call(functools.partial(kernel, n_wide, n_narrow), out_shape=tup...  21 us
    pallas_call x1, Pallas kernels, on_device(): pl.pallas_call(settle, out_shape=tuple((jax.ShapeDtypeStruct(shape, f32)...  0.72 us

profile of v4, /device:TPU:0, one launch (start us, length us, event | category | flops | bytes accessed | tf_op | source)
XLA Modules:
  0.0 22.4 jit_solution(12308791116574327675)
XLA Ops:
  0.6 21.0 %arnoldi.1 = (f32[2,4,64,128]{3,2,1,0:T(8,128)S(1)}, f32[2,18]{1,0:T(2,128)S(1)}) custom-call(f32[16]{0:T(128)} %coeffs_hbm.1, f32[16,64,512]{2,1,0:T(8,128)} %basis_hbm.1, f32[4,64,512]{2,1,0:T(8,128)} %geom_hbm.1, s32[6,64]{1,0:T(8,128)} %orient_hbm.1, bf16[512,256]{1,0:T(8,128)(2,1)} %constant.4.clone.packed_hbm, f32[64,128]{1,0:T(8,128)} %constant.5.clone.coef_hbm), custom_call_target="tpu_custom_call" | custom-call | tf_op jit(solution)/shard_map/arnoldi/pallas_call | solution.py:827
  21.7 0.7 %settle.1 = (f32[2,64,512]{2,1,0:T(8,128)}, f32[2,18]{1,0:T(2,128)}) custom-call(f32[2,4,64,128]{3,2,1,0:T(8,128)S(1)} %get-tuple-element.4.vectors, f32[2,18]{1,0:T(2,128)S(1)} %get-tuple-element.5.matrix), custom_call_target="tpu_custom_call" | custom-call | tf_op jit(solution)/shard_map/settle/pallas_call | solution.py:863

commit v5 on v4

--- a/solution.py
+++ b/solution.py
@@ -260,15 +260,15 @@
         greetings = greetings + there.astype(jnp.int32)
 
     def greet():
+        to_plane(barrier)
         to_layer(barrier, layer - 1, below)
-        to_higher(barrier)
         for there, shift in crossing:
 
             @pl.when(there)
             def _():
                 signal(barrier, (wide + shift, narrow))
 
-        to_plane(barrier)
+        to_higher(barrier)
 
     inbox[...] = jnp.zeros_like(inbox)
     greet()
@@ -768,8 +768,8 @@
     terms = jnp.concatenate([along_in * (found[0] - 2.0 * along), along_in * with_one], axis=0)
     terms = jnp.sum(terms, axis=1, keepdims=True)
 
+    scale_one = lax.rsqrt(one + epsilon)
     norm_one = jnp.sqrt(one + epsilon)
-    scale_one = 1.0 / norm_one
     self_two = cross * (scale_one * scale_one)
     for at in pieces:
         piece = first[at]
@@ -778,8 +778,8 @@
 
     square = whole + terms[0:1] + self_two * (2.0 * (terms[1:2] - cross) + self_two * one)
     square = jnp.maximum(square, 0.0) * (scale_one * scale_one)
+    scale_two = scale_one * lax.rsqrt(square + epsilon)
     norm_two = jnp.sqrt(square + epsilon)
-    scale_two = scale_one / norm_two
     for at in pieces:
         store_out(1, at, image[at] * scale_two)
 

time: 22.6 us -> 22.6 us (level)
  no operation moved by 1% of the time
where the time goes in v5:
time: 22.6 us; the launch traced here: 22.4 us
  Pallas kernels  21.8 us (96%)
  between operations  0.64 us (3%)
    pallas_call x1, Pallas kernels, on_device(): pl.pallas_call(functools.partial(kernel, n_wide, n_narrow), out_shape=tup...  21 us
    pallas_call x1, Pallas kernels, on_device(): pl.pallas_call(settle, out_shape=tuple((jax.ShapeDtypeStruct(shape, f32)...  0.72 us

profile of v5, /device:TPU:0, one launch (start us, length us, event | category | flops | bytes accessed | tf_op | source)
XLA Modules:
  0.0 22.4 jit_solution(13263967395724957505)
XLA Ops:
  0.6 21.0 %arnoldi.1 = (f32[2,4,64,128]{3,2,1,0:T(8,128)S(1)}, f32[2,18]{1,0:T(2,128)S(1)}) custom-call(f32[16]{0:T(128)} %coeffs_hbm.1, f32[16,64,512]{2,1,0:T(8,128)} %basis_hbm.1, f32[4,64,512]{2,1,0:T(8,128)} %geom_hbm.1, s32[6,64]{1,0:T(8,128)} %orient_hbm.1, bf16[512,256]{1,0:T(8,128)(2,1)} %constant.4.clone.packed_hbm, f32[64,128]{1,0:T(8,128)} %constant.5.clone.coef_hbm), custom_call_target="tpu_custom_call" | custom-call | tf_op jit(solution)/shard_map/arnoldi/pallas_call | solution.py:827
  21.7 0.7 %settle.1 = (f32[2,64,512]{2,1,0:T(8,128)}, f32[2,18]{1,0:T(2,128)}) custom-call(f32[2,4,64,128]{3,2,1,0:T(8,128)S(1)} %get-tuple-element.4.vectors, f32[2,18]{1,0:T(2,128)S(1)} %get-tuple-element.5.matrix), custom_call_target="tpu_custom_call" | custom-call | tf_op jit(solution)/shard_map/settle/pallas_call | solution.py:863

commit v6 on v5

--- a/solution.py
+++ b/solution.py
@@ -441,8 +441,10 @@
         ]
         outbox[step, 2] = faces(ends, pick_z)
 
+        early_parts = prepare(1) if step else None
+
         def inner_work():
-            parts = prepare(1)
+            parts = early_parts if step else prepare(1)
             rows = pl.ds(edge, elements - edge)
             found = local(
                 parts, rows, lambda: step or await_rows(geom, edge, elements - edge, 5)

time: 22.6 us -> 22.5 us (level)
  no operation moved by 1% of the time
where the time goes in v6:
time: 22.5 us; the launch traced here: 22.4 us
  Pallas kernels  21.7 us (96%)
  between operations  0.64 us (3%)
    pallas_call x1, Pallas kernels, on_device(): pl.pallas_call(functools.partial(kernel, n_wide, n_narrow), out_shape=tup...  21 us
    pallas_call x1, Pallas kernels, on_device(): pl.pallas_call(settle, out_shape=tuple((jax.ShapeDtypeStruct(shape, f32)...  0.72 us

profile of v6, /device:TPU:0, one launch (start us, length us, event | category | flops | bytes accessed | tf_op | source)
XLA Modules:
  0.0 22.4 jit_solution(17882915466663210190)
XLA Ops:
  0.6 21.0 %arnoldi.1 = (f32[2,4,64,128]{3,2,1,0:T(8,128)S(1)}, f32[2,18]{1,0:T(2,128)S(1)}) custom-call(f32[16]{0:T(128)} %coeffs_hbm.1, f32[16,64,512]{2,1,0:T(8,128)} %basis_hbm.1, f32[4,64,512]{2,1,0:T(8,128)} %geom_hbm.1, s32[6,64]{1,0:T(8,128)} %orient_hbm.1, bf16[512,256]{1,0:T(8,128)(2,1)} %constant.4.clone.packed_hbm, f32[64,128]{1,0:T(8,128)} %constant.5.clone.coef_hbm), custom_call_target="tpu_custom_call" | custom-call | tf_op jit(solution)/shard_map/arnoldi/pallas_call | solution.py:829
  21.6 0.7 %settle.1 = (f32[2,64,512]{2,1,0:T(8,128)}, f32[2,18]{1,0:T(2,128)}) custom-call(f32[2,4,64,128]{3,2,1,0:T(8,128)S(1)} %get-tuple-element.4.vectors, f32[2,18]{1,0:T(2,128)S(1)} %get-tuple-element.5.matrix), custom_call_target="tpu_custom_call" | custom-call | tf_op jit(solution)/shard_map/settle/pallas_call | solution.py:865

commit v7 on v5

--- a/solution.py
+++ b/solution.py
@@ -260,15 +260,15 @@
         greetings = greetings + there.astype(jnp.int32)
 
     def greet():
-        to_plane(barrier)
         to_layer(barrier, layer - 1, below)
+        to_higher(barrier)
         for there, shift in crossing:
 
             @pl.when(there)
             def _():
                 signal(barrier, (wide + shift, narrow))
 
-        to_higher(barrier)
+        to_plane(barrier)
 
     inbox[...] = jnp.zeros_like(inbox)
     greet()
@@ -772,9 +772,11 @@
     norm_one = jnp.sqrt(one + epsilon)
     self_two = cross * (scale_one * scale_one)
     for at in pieces:
+        image[at] = less_basis(image[at], parts, at)
+    for at in pieces:
         piece = first[at]
         store_out(0, at, piece * scale_one)
-        image[at] = less_basis(image[at] - self_two * piece, parts, at)
+        image[at] = image[at] - self_two * piece
 
     square = whole + terms[0:1] + self_two * (2.0 * (terms[1:2] - cross) + self_two * one)
     square = jnp.maximum(square, 0.0) * (scale_one * scale_one)

time: 22.6 us -> 22.6 us (level)
  no operation moved by 1% of the time
where the time goes in v7:
time: 22.6 us; the launch traced here: 22.4 us
  Pallas kernels  21.8 us (96%)
  between operations  0.64 us (3%)
    pallas_call x1, Pallas kernels, on_device(): pl.pallas_call(functools.partial(kernel, n_wide, n_narrow), out_shape=tup...  21.1 us
    pallas_call x1, Pallas kernels, on_device(): pl.pallas_call(settle, out_shape=tuple((jax.ShapeDtypeStruct(shape, f32)...  0.72 us

profile of v7, /device:TPU:0, one launch (start us, length us, event | category | flops | bytes accessed | tf_op | source)
XLA Modules:
  0.0 22.4 jit_solution(6019957506705251871)
XLA Ops:
  0.6 21.1 %arnoldi.1 = (f32[2,4,64,128]{3,2,1,0:T(8,128)S(1)}, f32[2,18]{1,0:T(2,128)S(1)}) custom-call(f32[16]{0:T(128)} %coeffs_hbm.1, f32[16,64,512]{2,1,0:T(8,128)} %basis_hbm.1, f32[4,64,512]{2,1,0:T(8,128)} %geom_hbm.1, s32[6,64]{1,0:T(8,128)} %orient_hbm.1, bf16[512,256]{1,0:T(8,128)(2,1)} %constant.4.clone.packed_hbm, f32[64,128]{1,0:T(8,128)} %constant.5.clone.coef_hbm), custom_call_target="tpu_custom_call" | custom-call | tf_op jit(solution)/shard_map/arnoldi/pallas_call | solution.py:829
  21.7 0.7 %settle.1 = (f32[2,64,512]{2,1,0:T(8,128)}, f32[2,18]{1,0:T(2,128)}) custom-call(f32[2,4,64,128]{3,2,1,0:T(8,128)S(1)} %get-tuple-element.4.vectors, f32[2,18]{1,0:T(2,128)S(1)} %get-tuple-element.5.matrix), custom_call_target="tpu_custom_call" | custom-call | tf_op jit(solution)/shard_map/settle/pallas_call | solution.py:865
